TPU v7x, 256 devices: a whole 4x4x8 slice. The times are simulated.
256 devices in a mesh: rows: 16 (over y_hi, z), pairs: 16 (over x, y_lo, core).
Axes of the slice: x: 4, y: 4 (y_hi: 2, y_lo: 2; y = y_hi * 2 + y_lo), z: 8, core: 2. Of those that a mesh axis runs over, the one named last changes fastest.
Arguments:
- matrix: float32 [32768, 8192], P('rows', 'pairs'), may hold values from -40 to 40
Outputs:
- rotated: float32 [32768, 8192], P('rows', 'pairs')
All inputs are finite; a program needn't handle non-finite values.
Results may differ from a plain program's by a relative error of at most 0.0001.
Values sent between devices are 32-bit elements; how exact they have to be, the bound alone decides.
No kernel may reach another device: no remote copies, remote signals or barrier semaphores. Data moves between devices by JAX's collectives and lax.ppermute only.
A program may use at most 64 MiB of HBM per device.

v0:
```python
import jax
import jax.numpy as jnp
from jax import lax
from jax.sharding import PartitionSpec as P

STEPS = 2


def filled_up(lines, length):
    spare = -len(lines) % length
    return jnp.pad(lines, [(0, spare)] + [(0, 0)] * (lines.ndim - 1))


def from_everyone(value, axis):
    copies = jnp.broadcast_to(value, (lax.axis_size(axis), *value.shape))
    return lax.all_to_all(copies, axis, split_axis=0, concat_axis=0, tiled=True)


def laid_out(blocks, dim):
    blocks = jnp.moveaxis(blocks, 0, dim)
    lengths = blocks.shape
    return blocks.reshape(*lengths[:dim], lengths[dim] * lengths[dim + 1], *lengths[dim + 2 :])


def collect(value, axis, dim):
    blocks = from_everyone(value, axis)
    return laid_out(blocks, dim)


def cut_along(value, dim, length):
    before, after = (value.shape[:dim], value.shape[dim + 1 :])
    return jnp.moveaxis(value.reshape(*before, length, -1, *after), dim, 0)


def summed_on_arrival(value, axis, dim):
    length = lax.axis_size(axis)
    blocks = lax.all_to_all(cut_along(value, dim, length), axis, 0, 0, tiled=True)
    return jnp.sum(blocks, axis=0)


def total_of(value, axes):
    padded = filled_up(value, lax.axis_size(axes))
    whole = collect(summed_on_arrival(padded, axes, 0), axes, 0)
    return lax.slice_in_dim(whole, 0, len(value)).reshape(value.shape)


def packed_total(arrays, axis):
    ravelled, at, done = (jnp.concatenate([a.reshape(-1) for a in arrays]), 0, [])
    subtotal = total_of(ravelled, axis)
    for a in arrays:
        done.append(subtotal[at : at + a.size].reshape(a.shape))
        at += a.size
    return tuple(done)


def passed_along(value, axis, by):
    length = lax.axis_size(axis)
    pairs = [(i, i + by) for i in range(length) if 0 <= i + by < length]
    return lax.ppermute(value, axis, pairs)


def spd_solve(system, right_side):
    factor = jnp.linalg.cholesky(system)
    middle = lax.linalg.triangular_solve(factor, right_side, left_side=True, lower=True)
    return lax.linalg.triangular_solve(factor, middle, left_side=True, lower=True, transpose_a=True)


def cayley_rotation(cross_block, norms_first, norms_second, rows_all):
    precise = lax.Precision.HIGHEST
    block_cols = cross_block.shape[0]
    scale_first = lax.rsqrt(norms_first / rows_all + 1e-06)
    scale_second = lax.rsqrt(norms_second / rows_all + 1e-06)
    coupling = 0.5 * cross_block * scale_first[:, None] * scale_second[None, :] / rows_all
    identity = jnp.eye(block_cols, dtype=jnp.float32)
    first_system = identity + jnp.dot(
        coupling, coupling.T, precision=precise, preferred_element_type=jnp.float32
    )
    first_sol = spd_solve(first_system, jnp.concatenate([identity, coupling], axis=1))
    lower_sol = jnp.dot(
        coupling.T, first_sol, precision=precise, preferred_element_type=jnp.float32
    )
    upper_rows = jnp.concatenate(
        [2.0 * first_sol[:, :block_cols] - identity, 2.0 * first_sol[:, block_cols:]], axis=1
    )
    lower_rows = jnp.concatenate(
        [-2.0 * lower_sol[:, :block_cols], identity - 2.0 * lower_sol[:, block_cols:]], axis=1
    )
    return jnp.concatenate([upper_rows, lower_rows], axis=0)


def shards(matrix):
    precise = lax.Precision.HIGHEST
    block_cols = matrix.shape[1] // 2
    rows_all = matrix.shape[0] * lax.axis_size("rows")
    position = lax.axis_index("pairs")
    cycle_size = lax.axis_size("pairs")
    first_block = matrix[:, :block_cols]
    second_block = matrix[:, block_cols:]
    for turn_index in range(STEPS):
        both = jnp.concatenate([first_block, second_block], axis=1)
        cross_local = lax.dot_general(
            first_block,
            second_block,
            (((0,), (0,)), ((), ())),
            precision=precise,
            preferred_element_type=jnp.float32,
        )
        first_local = jnp.sum(first_block * first_block, axis=0)
        second_local = jnp.sum(second_block * second_block, axis=0)
        cross_block, norms_first, norms_second = packed_total(
            (cross_local, first_local, second_local), "rows"
        )
        rotate = cayley_rotation(cross_block, norms_first, norms_second, rows_all)
        turned = jnp.dot(both, rotate, precision=precise, preferred_element_type=jnp.float32)
        first_block = turned[:, :block_cols]
        second_block = turned[:, block_cols:]
        outgoing = jnp.where(position == 0, second_block, first_block)
        from_lower = passed_along(outgoing, "pairs", 1)
        from_upper = passed_along(second_block, "pairs", -1)
        next_first = jnp.where(position == 0, first_block, from_lower)
        second_block = jnp.where(position == cycle_size - 1, first_block, from_upper)
        first_block = next_first
    return jnp.concatenate([first_block, second_block], axis=1)


def solution(mesh):
    return jax.shard_map(
        shards,
        mesh=mesh,
        in_specs=(P("rows", "pairs"),),
        out_specs=P("rows", "pairs"),
        check_vma=False,
    )
```

profile of v0, /device:TPU:44, one launch (start us, length us, event | category | flops | bytes accessed | tf_op | source)
XLA Modules:
  0.0 346.7 jit_solution(2272736608737753764)
XLA Ops:
  0.0 2.7 multiply_reduce_fusion.3
  2.7 0.8 copy-done
  3.5 3.6 %fusion.7 = f32[32,2,8,128]{3,2,1,0:T(8,128)S(1)} fusion(f32[2048,512]{1,0:T(8,128)S(1)} %copy-done), kind=kOutput, calls=%fused_computation.29 | convolution fusion | flops 1610612736 | bytes 4456448 | tf_op jit(solution)/shard_map/dot_general | solution.py:101
  7.2 1.1 all_to_all.20
  8.3 10.3 %all-to-all-start = ((f32[16,1,4128]{2,1,0:T(1,128)}), f32[16,1,4128]{2,1,0:T(1,128)S(1)}, u32[]{:S(2)}, u32[]{:S(2)}) async-start(f32[16,1,4128]{2,1,0:T(1,128)} %all_to_all.20), calls=%async_computation | async-start | bytes 540672 | tf_op jit(solution)/shard_map/all_to_all | solution.py:37
  18.6 11.6 %all-to-all-done = f32[16,1,4128]{2,1,0:T(1,128)S(1)} async-done(((f32[16,1,4128]{2,1,0:T(1,128)}), f32[16,1,4128]{2,1,0:T(1,128)S(1)}, u32[]{:S(2)}, u32[]{:S(2)}) %all-to-all-start) | async-done | bytes 264224 | tf_op jit(solution)/shard_map/all_to_all | solution.py:37
  30.4 0.8 broadcast_in_dim.5
  31.2 4.9 %all-to-all-start.1 = ((f32[16,1,4128]{2,1,0:T(1,128)}), f32[16,1,4128]{2,1,0:T(1,128)S(1)}, u32[]{:S(2)}, u32[]{:S(2)}) async-start(f32[16,1,4128]{2,1,0:T(1,128)} %broadcast_in_dim.5), calls=%async_computation.1 | async-start | bytes 540672 | tf_op jit(solution)/shard_map/all_to_all | solution.py:16
  36.2 11.2 %all-to-all-done.1 = f32[16,1,4128]{2,1,0:T(1,128)S(1)} async-done(((f32[16,1,4128]{2,1,0:T(1,128)}), f32[16,1,4128]{2,1,0:T(1,128)S(1)}, u32[]{:S(2)}, u32[]{:S(2)}) %all-to-all-start.1) | async-done | bytes 264224 | tf_op jit(solution)/shard_map/all_to_all | solution.py:16
  47.3 0.6 reduce.10
  49.4 11.7 %cholesky.130 = f32[128,128]{1,0:T(8,128)S(1)} custom-call(f32[128,128]{1,0:T(8,128)S(1)} %cholesky.194), custom_call_target="Cholesky" | custom-call | tf_op jit(solution)/shard_map/jit(cholesky)/cholesky | solution.py:63
  61.1 9.8 %custom-call.17 = f32[1,128,128]{1,2,0:T(8,128)S(1)} custom-call(f32[1,128,128]{2,1,0:T(8,128)S(1)} %get-tuple-element.93), custom_call_target="InvertDiagBlocksLowerTriangular" | custom-call | tf_op jit(solution)/shard_map/jit(cholesky)/cholesky | solution.py:63
  71.4 11.7 %cholesky.147 = f32[128,128]{1,0:T(8,128)S(1)} custom-call(f32[128,128]{1,0:T(8,128)S(1)} %convolution_subtract_fusion.5), custom_call_target="Cholesky" | custom-call | tf_op jit(solution)/shard_map/jit(cholesky)/cholesky | solution.py:63
  83.2 0.6 compare_reduce_fusion.2
  85.6 3.8 %while.8 = (s32[]{:T(128)}, f32[256,256]{1,0:T(8,128)S(1)}, s32[2,2]{1,0:T(2,128)S(1)}, f32[2,128,128]{2,1,0:T(8,128)S(1)}, s32[]{:T(128)}) while((s32[]{:T(128)}, f32[256,256]{1,0:T(8,128)S(1)}, s32[2,2]{1,0:T(2,128)S(1)}, f32[2,128,128]{2,1,0:T(8,128)S(1)}, s32[]{:T(128)}) %tuple.65), condition=%wide.while_cond.1, body=%wide.while_body.1.sunk | while | flops 2 | bytes 131181 | solution.py:65
  86.2 1.3 bitcast_dynamic-update-slice_fusion.4
  88.1 1.3 bitcast_dynamic-update-slice_fusion.4
  89.4 19.7 %custom-call.19 = f32[2,128,128]{1,2,0:T(8,128)S(1)} custom-call(f32[2,128,128]{2,1,0:T(8,128)S(1)} %get-tuple-element.37), custom_call_target="InvertDiagBlocksLowerTriangular" | custom-call | tf_op jit(solution)/shard_map/triangular_solve/custom-call.4 | solution.py:65
  112.8 8.8 %convolution_bitcast_fusion = f32[2048,512]{0,1:T(8,128)S(1)} fusion(f32[2048,512]{1,0:T(8,128)} %param.6, f32[256,256]{0,1:T(8,128)S(1)} %get-tuple-element.81, f32[256,256]{0,1:T(8,128)S(1)} %get-tuple-element.80, f32[256,256]{0,1:T(8,128)S(1)} %get-tuple-element.79, f32[256,256]{0,1:T(8,128)S(1)} %get-tuple-element.78), kind=kOutput, calls=%fused_computation.9 | convolution fusion | flops 6443237376 | bytes 9437184 | tf_op jit(solution)/shard_map/dot_general | solution.py:114
  121.6 2.4 slice_select_fusion.5
  124.1 0.8 copy-done.1
  124.9 1.9 collective-permute-start
  126.8 3.6 %collective-permute-start.1 = (f32[2048,256]{0,1:T(8,128)}, f32[2048,256]{0,1:T(8,128)}, u32[]{:S(2)}, u32[]{:S(2)}) collective-permute-start(f32[2048,256]{0,1:T(8,128)} %get-tuple-element.73), channel_id=1, source_target_pairs={{1,0},{2,1},{3,2},{4,3},{5,4},{6,5},{7,6},{8,7},{9,8},{10,9},{11,1... | collective-permute-start | bytes 6291464 | tf_op jit(solution)/shard_map/ppermute | solution.py:59
  130.5 45.9 %collective-permute-done = f32[2048,256]{0,1:T(8,128)S(1)} collective-permute-done((f32[2048,256]{0,1:T(8,128)}, f32[2048,256]{0,1:T(8,128)S(1)}, u32[]{:S(2)}, u32[]{:S(2)}) %collective-permute-start) | collective-permute-done | bytes 2097184 | tf_op jit(solution)/shard_map/ppermute | solution.py:59
  176.4 1.3 copy-done.4
  177.7 3.4 multiply_reduce_fusion.1
  181.1 1.9 convolution_bitcast_fusion.1
  183.6 15.0 %all_to_all.30 = f32[16,1,4128]{2,1,0:T(1,128)S(1)} all-to-all(f32[16,1,4128]{2,1,0:T(1,128)S(1)} %all_to_all.23), channel_id=1, replica_groups=mesh['rows'=16,'pairs'=16] {'rows'}, dimensions={0} | all-to-all | bytes 528384 | tf_op jit(solution)/shard_map/all_to_all | solution.py:37
  198.9 14.6 %all_to_all.31 = f32[16,1,4128]{2,1,0:T(1,128)S(1)} all-to-all(f32[16,1,4128]{2,1,0:T(1,128)S(1)} %broadcast_in_dim.6), channel_id=1, replica_groups=mesh['rows'=16,'pairs'=16] {'rows'}, dimensions={0} | all-to-all | bytes 528384 | tf_op jit(solution)/shard_map/all_to_all | solution.py:16
  213.5 0.6 reduce.12
  215.6 11.7 %cholesky.164 = f32[128,128]{1,0:T(8,128)S(1)} custom-call(f32[128,128]{1,0:T(8,128)S(1)} %cholesky.197), custom_call_target="Cholesky" | custom-call | tf_op jit(solution)/shard_map/jit(cholesky)/cholesky | solution.py:63
  227.3 9.8 %custom-call.20 = f32[1,128,128]{1,2,0:T(8,128)S(1)} custom-call(f32[1,128,128]{2,1,0:T(8,128)S(1)} %get-tuple-element.89), custom_call_target="InvertDiagBlocksLowerTriangular" | custom-call | tf_op jit(solution)/shard_map/jit(cholesky)/cholesky | solution.py:63
  237.6 11.7 %cholesky.181 = f32[128,128]{1,0:T(8,128)S(1)} custom-call(f32[128,128]{1,0:T(8,128)S(1)} %convolution_subtract_fusion.4), custom_call_target="Cholesky" | custom-call | tf_op jit(solution)/shard_map/jit(cholesky)/cholesky | solution.py:63
  249.4 0.6 compare_reduce_fusion
  250.0 0.7 compare_reduce_fusion.1
  252.0 4.1 %while.9 = (s32[]{:T(128)}, f32[256,256]{1,0:T(8,128)S(1)}, s32[2,2]{1,0:T(2,128)S(1)}, f32[2,128,128]{2,1,0:T(8,128)S(1)}, s32[]{:T(128)}) while((s32[]{:T(128)}, f32[256,256]{1,0:T(8,128)S(1)}, s32[2,2]{1,0:T(2,128)S(1)}, f32[2,128,128]{2,1,0:T(8,128)S(1)}, s32[]{:T(128)}) %tuple.71), condition=%wide.while_cond.1.clone, body=%wide.while_body.1.clone.sunk | while | flops 2 | bytes 131181 | solution.py:65
  252.1 0.7 fusion.105
  252.7 1.3 bitcast_dynamic-update-slice_fusion.5
  254.1 0.7 fusion.105
  254.8 1.3 bitcast_dynamic-update-slice_fusion.5
  256.1 19.9 %custom-call.22 = f32[2,128,128]{1,2,0:T(8,128)S(1)} custom-call(f32[2,128,128]{2,1,0:T(8,128)S(1)} %get-tuple-element.39), custom_call_target="InvertDiagBlocksLowerTriangular" | custom-call | tf_op jit(solution)/shard_map/triangular_solve/custom-call.4 | solution.py:65
  280.0 7.5 %fusion = f32[2048,512]{0,1:T(8,128)S(1)} fusion(f32[2048,256]{0,1:T(8,128)S(1)} %copy-done.3, f32[2048,256]{0,1:T(8,128)S(1)} %get-tuple-element.59, f32[256,256]{0,1:T(8,128)S(1)} %get-tuple-element.77, f32[256,256]{0,1:T(8,128)S(1)} %get-tuple-element.76, f32[256,256]{0,1:T(8,128)S(1)} %get-tuple-element.75, f32[256,256]{0,1:T(8,128)S(1)} %get-tuple-element.74), kind=kOutput, calls=%fused_computation.4 | convolution fusion | flops 6444285952 | bytes 9437184 | tf_op jit(solution)/shard_map/dot_general | solution.py:114
  288.1 1.9 collective-permute-start.2
  290.0 3.6 %collective-permute-start.3 = (f32[2048,256]{0,1:T(8,128)S(1)}, f32[2048,256]{0,1:T(8,128)S(1)}, u32[]{:S(2)}, u32[]{:S(2)}) collective-permute-start(f32[2048,256]{0,1:T(8,128)S(1)} %get-tuple-element.69), channel_id=1, source_target_pairs={{1,0},{2,1},{3,2},{4,3},{5,4},{6,5},{7,6},{8,7},{9,8},{10,9},{11,1... | collective-permute-start | bytes 6291464 | tf_op jit(solution)/shard_map/ppermute | solution.py:59
  293.6 44.2 %collective-permute-done.2 = f32[2048,256]{0,1:T(8,128)S(1)} collective-permute-done((f32[2048,256]{0,1:T(8,128)S(1)}, f32[2048,256]{0,1:T(8,128)S(1)}, u32[]{:S(2)}, u32[]{:S(2)}) %collective-permute-start.2) | collective-permute-done | bytes 2097184 | tf_op jit(solution)/shard_map/ppermute | solution.py:59
  337.9 0.8 slice_select_fusion.1
  338.7 2.4 pad_maximum_fusion
  341.2 5.3 %copy.82 = f32[2048,512]{1,0:T(8,128)} copy(f32[2048,512]{0,1:T(8,128)} %pad_maximum_fusion) | data formatting | bytes 8388608 | tf_op jit(solution)/shard_map/concatenate | solution.py:123
  (81 shorter events, 14.8 us)
Async XLA Ops:
  0.0 3.4 copy-start
  8.3 21.9 %all-to-all-start = ((f32[16,1,4128]{2,1,0:T(1,128)}), f32[16,1,4128]{2,1,0:T(1,128)S(1)}, u32[]{:S(2)}, u32[]{:S(2)}) async-start(f32[16,1,4128]{2,1,0:T(1,128)} %all_to_all.20), calls=%async_computation | async-start | bytes 540672 | tf_op jit(solution)/shard_map/all_to_all | solution.py:37
  31.2 16.1 %all-to-all-start.1 = ((f32[16,1,4128]{2,1,0:T(1,128)}), f32[16,1,4128]{2,1,0:T(1,128)S(1)}, u32[]{:S(2)}, u32[]{:S(2)}) async-start(f32[16,1,4128]{2,1,0:T(1,128)} %broadcast_in_dim.5), calls=%async_computation.1 | async-start | bytes 540672 | tf_op jit(solution)/shard_map/all_to_all | solution.py:16
  121.6 3.3 copy-start.1
  124.9 51.5 %collective-permute-start = (f32[2048,256]{0,1:T(8,128)}, f32[2048,256]{0,1:T(8,128)S(1)}, u32[]{:S(2)}, u32[]{:S(2)}) collective-permute-start(f32[2048,256]{0,1:T(8,128)} %get-tuple-element.72), channel_id=1, source_target_pairs={{0,1},{1,2},{2,3},{3,4},{4,5},{5,6},{6,7},{7,8},{8,9},{9,10},{10,1... | collective-permute-start | bytes 6291464 | tf_op jit(solution)/shard_map/ppermute | solution.py:59
  126.8 50.9 %collective-permute-start.1 = (f32[2048,256]{0,1:T(8,128)}, f32[2048,256]{0,1:T(8,128)}, u32[]{:S(2)}, u32[]{:S(2)}) collective-permute-start(f32[2048,256]{0,1:T(8,128)} %get-tuple-element.73), channel_id=1, source_target_pairs={{1,0},{2,1},{3,2},{4,3},{5,4},{6,5},{7,6},{8,7},{9,8},{10,9},{11,1... | collective-permute-start | bytes 6291464 | tf_op jit(solution)/shard_map/ppermute | solution.py:59
  176.4 1.3 copy-start.4
  181.1 1.9 copy-start.2
  278.4 1.6 copy-start.3
  288.1 49.8 %collective-permute-start.2 = (f32[2048,256]{0,1:T(8,128)S(1)}, f32[2048,256]{0,1:T(8,128)S(1)}, u32[]{:S(2)}, u32[]{:S(2)}) collective-permute-start(f32[2048,256]{0,1:T(8,128)S(1)} %get-tuple-element.68), channel_id=1, source_target_pairs={{0,1},{1,2},{2,3},{3,4},{4,5},{5,6},{6,7},{7,8},{8,9},{9,10},{10,1... | collective-permute-start | bytes 6291464 | tf_op jit(solution)/shard_map/ppermute | solution.py:59
  290.0 47.9 %collective-permute-start.3 = (f32[2048,256]{0,1:T(8,128)S(1)}, f32[2048,256]{0,1:T(8,128)S(1)}, u32[]{:S(2)}, u32[]{:S(2)}) collective-permute-start(f32[2048,256]{0,1:T(8,128)S(1)} %get-tuple-element.69), channel_id=1, source_target_pairs={{1,0},{2,1},{3,2},{4,3},{5,4},{6,5},{7,6},{8,7},{9,8},{10,9},{11,1... | collective-permute-start | bytes 6291464 | tf_op jit(solution)/shard_map/ppermute | solution.py:59
where the time goes:
time: 351 us; the launch traced here: 347 us
  other arithmetic  123 us (35%)
  waiting for transfers between devices  113 us (32%)
  matrix products  30.8 us (9%)
  blocking collectives  29.6 us (8%)
  starting transfers between devices  26.3 us (7%)
  local copies, waits for them, and re-layouts  20.6 us (6%)
    ppermute x4, waiting for transfers between devices, passed_along(): return lax.ppermute(value, axis, pairs)  90.1 us
    another operation x13, other arithmetic, spd_solve(): factor = jnp.linalg.cholesky(system)  68.6 us
    another operation x5, other arithmetic, spd_solve(): lax.linalg.triangular_solve(factor, middle, left_side=True, lower=True, t...  40 us
    dot_general x2, matrix products, shards(): jnp.dot(both, rotate, precision=precise, preferred_element_type=jnp.float32)  16.3 us
    all_to_all x1, blocking collectives, summed_on_arrival(): lax.all_to_all(cut_along(value, dim, length), axis, 0, 0, tiled=True)  15 us
    all_to_all x1, blocking collectives, from_everyone(): return lax.all_to_all(copies, axis, split_axis=0, concat_axis=0, tiled=True)  14.6 us
    all_to_all x1, waiting for transfers between devices, summed_on_arrival(): lax.all_to_all(cut_along(value, dim, length), axis, 0, 0, tiled=True)  11.6 us
    all_to_all x1, waiting for transfers between devices, from_everyone(): return lax.all_to_all(copies, axis, split_axis=0, concat_axis=0, tiled=True)  11.2 us
  transfers between devices with their start and end apart: 6, of which 4 were waited for; matrix products, arithmetic and copies ran while one was open for 0% of the time, Pallas kernels for 0%

commit v1 on v0

v1 whole, which is shorter than its diff:
```python
import jax
import jax.numpy as jnp
from jax import lax
from jax.experimental import pallas as pl
from jax.experimental.pallas import tpu as pltpu
from jax.sharding import PartitionSpec as P

F32, BF16 = jnp.float32, jnp.bfloat16
TAIL = 8
LANES = 128


def halves(x):
    high = x.astype(BF16)
    return high, (x - high.astype(F32)).astype(BF16)


def product(a, b, dims=((1,), (0,))):
    return lax.dot_general(a, b, (dims, ((), ())), preferred_element_type=F32)


def three_products(a, b, dims=((1,), (0,))):
    (a_high, a_low), (b_high, b_low) = halves(a), halves(b)
    return product(a_high, b_high, dims) + (product(a_high, b_low, dims) + product(a_low, b_high, dims))


def full_product(a, b, dims=((1,), (0,))):
    return lax.dot_general(
        a, b, (dims, ((), ())), precision=lax.Precision.HIGHEST, preferred_element_type=F32
    )


def gram(left, left_at, right, right_at, peers, cols, block=512):
    per, wide = cols // peers, cols // LANES

    def kernel(left_ref, right_ref, out_ref, acc_ref, norms_ref):
        step = pl.program_id(0)

        @pl.when(step == 0)
        def _():
            acc_ref[...] = jnp.zeros_like(acc_ref)
            norms_ref[...] = jnp.zeros_like(norms_ref)

        a, b = left_ref[...], right_ref[...]
        acc_ref[...] += three_products(a, b, ((0,), (0,)))
        norms_ref[:, :cols] += jnp.sum((a * a).reshape(block // 8, 8, cols), axis=0)
        norms_ref[:, cols:] += jnp.sum((b * b).reshape(block // 8, 8, cols), axis=0)

        @pl.when(step == pl.num_programs(0) - 1)
        def _():
            total = jnp.sum(norms_ref[...], axis=0, keepdims=True)
            lines = [total[:, LANES * q : LANES * (q + 1)] for q in range(2 * wide)]
            tail = jnp.concatenate([*lines, jnp.zeros((TAIL - 2 * wide, LANES), F32)], axis=0)
            for peer in range(peers):
                rows = acc_ref[peer * per : (peer + 1) * per, :]
                for q in range(wide):
                    out_ref[peer, q * per : (q + 1) * per, :] = rows[:, LANES * q : LANES * (q + 1)]
                out_ref[peer, wide * per :, :] = tail

    shape = (peers, wide * per + TAIL, LANES)
    return pl.pallas_call(
        kernel,
        grid=(left.shape[0] // block,),
        in_specs=[
            pl.BlockSpec((block, cols), lambda i: (i, left_at)),
            pl.BlockSpec((block, cols), lambda i: (i, right_at)),
        ],
        out_specs=pl.BlockSpec(shape, lambda i: (0, 0, 0)),
        out_shape=jax.ShapeDtypeStruct(shape, F32),
        scratch_shapes=[pltpu.VMEM((cols, cols), F32), pltpu.VMEM((8, 2 * cols), F32)],
        name="gram",
    )(left, right)


def slab_sum(slabs, cols):
    peers = slabs.shape[0]
    per, wide = cols // peers, cols // LANES

    def kernel(in_ref, out_ref):
        total = in_ref[0]
        for peer in range(1, peers):
            total = total + in_ref[peer]
        rows = [total[q * per : (q + 1) * per] for q in range(wide)]
        out_ref[:per] = jnp.concatenate(rows, axis=1)
        tail = total[wide * per :]
        for side in range(2):
            lines = [tail[side * wide + q : side * wide + q + 1] for q in range(wide)]
            out_ref[per + side : per + side + 1] = jnp.concatenate(lines, axis=1)
        out_ref[per + 2 :] = jnp.zeros((TAIL - 2, cols), F32)

    return pl.pallas_call(
        kernel, out_shape=jax.ShapeDtypeStruct((per + TAIL, cols), F32), name="slab_sum"
    )(slabs)


def cayley(cross, norms, sign, rows_all, power_ref, inverse_ref):
    cols = cross.shape[0]
    scale_left = lax.rsqrt(norms[0:1] / rows_all + 1e-06)
    scale_right = lax.rsqrt(norms[1:2] / rows_all + 1e-06)
    row_at = lax.broadcasted_iota(jnp.int32, (cols, cols), 0)
    col_at = lax.broadcasted_iota(jnp.int32, (cols, cols), 1)
    diagonal = row_at == col_at
    identity = jnp.where(diagonal, 1.0, 0.0).astype(F32)
    spread = jnp.where(diagonal, jnp.broadcast_to(scale_left, (cols, cols)), 0.0)
    scale_left = jnp.sum(spread, axis=1, keepdims=True)
    coupling = (0.5 * sign) * cross * scale_left * scale_right / rows_all
    system = identity + full_product(coupling, coupling, ((1,), (1,)))
    bound = jnp.max(jnp.sum(jnp.abs(system), axis=0, keepdims=True))
    factor = 2.0 / (1.0 + bound)
    power = identity - factor * system
    inverse_ref[...] = factor * (identity + power)
    power_ref[...] = power
    ratio = (bound - 1.0) / (bound + 1.0)

    def more(carry):
        left, count = carry
        return (left > 1e-3) & (count < 40)

    def double(carry):
        left, count = carry
        before = power_ref[...]
        squared = three_products(before, before)
        power_ref[...] = squared
        inverse = inverse_ref[...]
        inverse_ref[...] = inverse + three_products(inverse, squared)
        return left * left, count + 1

    lax.while_loop(more, double, (ratio * ratio, jnp.int32(0)))

    def newton(_, carry):
        inverse = inverse_ref[...]
        inverse_ref[...] = inverse + full_product(inverse, identity - full_product(system, inverse))
        return carry

    lax.fori_loop(0, jnp.where(bound < 8.0, 1, 3), newton, 0)
    inverse = inverse_ref[...]
    upper = full_product(inverse, coupling)
    lower = full_product(coupling, upper, ((0,), (0,)))
    return 2.0 * inverse - identity, 2.0 * upper, -2.0 * upper.T, identity - 2.0 * lower


def store_halves(high_ref, low_ref, at_row, at_col, value):
    rows, cols = value.shape
    high, low = halves(value)
    high_ref[at_row : at_row + rows, at_col : at_col + cols] = high
    low_ref[at_row : at_row + rows, at_col : at_col + cols] = low


def step_one_matrices(gathered, norms, swap, rows_all):
    cols = gathered.shape[2]

    def kernel(swap_ref, cross_ref, norms_ref, high_ref, low_ref, power_ref, inverse_ref):
        cross = cross_ref[...].reshape(cols, cols)
        blocks = cayley(cross, norms_ref[...], 1.0, rows_all, power_ref, inverse_ref)
        turned = swap_ref[0] != 0
        for line in range(2):
            near, far = blocks[2 * line], blocks[2 * line + 1]
            store_halves(high_ref, low_ref, line * cols, 0, jnp.where(turned, far, near))
            store_halves(high_ref, low_ref, line * cols, cols, jnp.where(turned, near, far))

    out = jax.ShapeDtypeStruct((2 * cols, 2 * cols), BF16)
    vmem = pl.BlockSpec(memory_space=pltpu.VMEM)
    return pl.pallas_call(
        kernel,
        in_specs=[pl.BlockSpec(memory_space=pltpu.SMEM), vmem, vmem],
        out_shape=(out, out),
        scratch_shapes=[pltpu.VMEM((cols, cols), F32)] * 2,
        name="cayley_one",
    )(swap, gathered, norms)


def step_two_matrices(gathered, norms, other_norms, marks, rows_all):
    peers, both, cols = gathered.shape
    per = both // 2

    def kernel(marks_ref, cross_ref, norms_ref, other_ref, *refs):
        outs, (power_ref, inverse_ref) = refs[:4], refs[4:]
        for edge in range(2):
            cross = cross_ref[:, edge * per : (edge + 1) * per, :].reshape(cols, cols)
            sign = jnp.where(marks_ref[2 * edge] != 0, 1.0, -1.0).astype(F32)
            lines = (norms_ref, other_ref)[edge][...]
            blocks = cayley(cross, lines, sign, rows_all, power_ref, inverse_ref)
            moved_role = marks_ref[2 * edge + 1] != 0
            for line in range(2):
                value = jnp.where(moved_role, blocks[2 * line], blocks[2 * line + 1])
                store_halves(outs[2 * edge], outs[2 * edge + 1], line * cols, 0, value)

    out = jax.ShapeDtypeStruct((2 * cols, cols), BF16)
    vmem = pl.BlockSpec(memory_space=pltpu.VMEM)
    return pl.pallas_call(
        kernel,
        in_specs=[pl.BlockSpec(memory_space=pltpu.SMEM), vmem, vmem, vmem],
        out_shape=(out,) * 4,
        scratch_shapes=[pltpu.VMEM((cols, cols), F32)] * 2,
        name="cayley_two",
    )(marks, gathered, norms, other_norms)


def rotate(both, high, low, block=256):
    rows, width = both.shape
    cols = width // 2

    def kernel(x_ref, high_ref, low_ref, first_ref, second_ref):
        x_high, x_low = halves(x_ref[...])
        turned = product(x_high, high_ref[...]) + (
            product(x_high, low_ref[...]) + product(x_low, high_ref[...])
        )
        first_ref[...] = turned[:, :cols]
        second_ref[...] = turned[:, cols:]

    fixed = pl.BlockSpec((width, width), lambda i: (0, 0))
    half = pl.BlockSpec((block, cols), lambda i: (i, 0))
    return pl.pallas_call(
        kernel,
        grid=(rows // block,),
        in_specs=[pl.BlockSpec((block, width), lambda i: (i, 0)), fixed, fixed],
        out_specs=(half, half),
        out_shape=(jax.ShapeDtypeStruct((rows, cols), F32),) * 2,
        name="rotate",
    )(both, high, low)


def combine(at, left, right, high, low, before=None, block=256):
    rows, cols = left.shape

    def kernel(at_ref, left_ref, right_ref, high_ref, low_ref, *refs):
        out_ref = refs[-1]
        total = jnp.zeros((block, cols), F32)
        for line, ref in enumerate((left_ref, right_ref)):
            x_high, x_low = halves(ref[...])
            m_high = high_ref[line * cols : (line + 1) * cols, :]
            m_low = low_ref[line * cols : (line + 1) * cols, :]
            total += product(x_high, m_high) + (product(x_high, m_low) + product(x_low, m_high))
        out_ref[...] = total

    data = pl.BlockSpec((block, cols), lambda i, at_ref: (i, 0))
    fixed = pl.BlockSpec((2 * cols, cols), lambda i, at_ref: (0, 0))
    operands = [at, left, right, high, low]
    in_specs = [data, data, fixed, fixed]
    aliases = {}
    if before is not None:
        operands.append(before)
        in_specs.append(pl.BlockSpec(memory_space=pl.ANY))
        aliases = {len(operands) - 1: 0}
    return pl.pallas_call(
        kernel,
        grid_spec=pltpu.PrefetchScalarGridSpec(
            num_scalar_prefetch=1,
            grid=(rows // block,),
            in_specs=in_specs,
            out_specs=pl.BlockSpec((block, cols), lambda i, at_ref: (i, at_ref[0])),
        ),
        out_shape=jax.ShapeDtypeStruct((rows, 2 * cols), F32),
        input_output_aliases=aliases,
        name="combine",
    )(*operands)


def exchanged(blocks):
    return lax.all_to_all(blocks, "rows", 0, 0, tiled=True)


def shards(matrix):
    cols = matrix.shape[1] // 2
    peers = lax.axis_size("rows")
    rows_all = matrix.shape[0] * peers
    per = cols // peers
    position = lax.axis_index("pairs")
    size = lax.axis_size("pairs")
    ring = [*range(0, size, 2), *range(size - 1, 0, -2)]
    clockwise = [(ring[i], ring[(i + 1) % size]) for i in range(size)]
    back = [(b, a) for a, b in clockwise]
    even = position % 2 == 0

    slabs = exchanged(gram(matrix, 0, matrix, 1, peers, cols))
    mine = slab_sum(slabs, cols)
    gathered = exchanged(jnp.broadcast_to(mine[:per], (peers, per, cols)))
    swap = jnp.where(even & (position > 0), 0, 1).astype(jnp.int32)[None]
    high, low = step_one_matrices(gathered, mine[per:], swap, float(rows_all))
    onward, kept = rotate(matrix, high, low)

    arrived = lax.ppermute(onward, "pairs", clockwise)
    kept_late, arrived = lax.optimization_barrier((kept, arrived))
    returned = lax.ppermute(kept_late, "pairs", back)
    slabs = exchanged(gram(arrived, 0, kept, 0, peers, cols))
    mine = slab_sum(slabs, cols)
    other = lax.ppermute(mine, "pairs", back)
    pair = jnp.concatenate([mine[:per], other[:per]], axis=0)
    gathered = exchanged(jnp.broadcast_to(pair, (peers, 2 * per, cols)))
    marks = jnp.stack(
        [
            (even & (position > 0)) | (position == size - 1),
            position != 0,
            even,
            position == 1,
        ]
    ).astype(jnp.int32)
    matrices = step_two_matrices(gathered, mine[per:], other[per:], marks, float(rows_all))
    in_first = jnp.where(even, 0, 1).astype(jnp.int32)[None]
    half_done = combine(in_first, arrived, kept, *matrices[:2])
    return combine(1 - in_first, onward, returned, *matrices[2:], before=half_done)


def solution(mesh):
    return jax.shard_map(
        shards,
        mesh=mesh,
        in_specs=(P("rows", "pairs"),),
        out_specs=P("rows", "pairs"),
        check_vma=False,
    )
```

time: 351 us -> 225 us (0.64)
  the two profiles are of different devices: /device:TPU:44 before, /device:TPU:2 now
where the time goes in v1:
time: 225 us; the launch traced here: 224 us
  waiting for transfers between devices  70.9 us (32%)
  Pallas kernels  60.8 us (27%)
  blocking collectives  42.2 us (19%)
  starting transfers between devices  41.4 us (18%)
  local copies, waits for them, and re-layouts  7.72 us (3%)
    ppermute x1, waiting for transfers between devices, shards(): arrived = lax.ppermute(onward, 'pairs', clockwise)  44.4 us
    all_to_all x2, blocking collectives, exchanged(): return lax.all_to_all(blocks, 'rows', 0, 0, tiled=True)  42.2 us
    ppermute x1, starting transfers between devices, shards(): returned = lax.ppermute(kept_late, 'pairs', back)  23 us
    all_to_all x2, waiting for transfers between devices, exchanged(): return lax.all_to_all(blocks, 'rows', 0, 0, tiled=True)  22.4 us
    pallas_call x1, Pallas kernels, step_two_matrices(): pl.pallas_call(kernel, in_specs=[pl.BlockSpec(memory_space=pltpu.SMEM), v...  17.3 us
    pallas_call x2, Pallas kernels, combine(): pl.pallas_call(kernel, grid_spec=pltpu.PrefetchScalarGridSpec(num_scalar_...  15 us
    all_to_all x2, starting transfers between devices, exchanged(): return lax.all_to_all(blocks, 'rows', 0, 0, tiled=True)  13.2 us
    pallas_call x2, Pallas kernels, gram(): pl.pallas_call(kernel, grid=(left.shape[0] // block,), in_specs=[pl.Block...  9.33 us
  transfers between devices with their start and end apart: 5, of which 4 were waited for; matrix products, arithmetic and copies ran while one was open for 2% of the time, Pallas kernels for 14%

profile of v1, /device:TPU:2, one launch (start us, length us, event | category | flops | bytes accessed | tf_op | source)
XLA Modules:
  0.0 223.7 jit_solution(18038216898980499782)
XLA Ops:
  0.0 4.7 %gram.2 = f32[16,40,128]{2,1,0:T(8,128)} custom-call(f32[2048,512]{1,0:T(8,128)} %x_ref.1, f32[2048,512]{1,0:T(8,128)} %x_ref.1), custom_call_target="tpu_custom_call" | custom-call | tf_op jit(solution)/shard_map/gram/pallas_call | solution.py:61
  4.7 24.2 %all_to_all.20.in_ref = f32[16,40,128]{2,1,0:T(8,128)} all-to-all(f32[16,40,128]{2,1,0:T(8,128)} %gram.2), channel_id=1, replica_groups=mesh['rows'=16,'pairs'=16] {'rows'}, dimensions={0} | all-to-all | bytes 655360 | tf_op jit(solution)/shard_map/all_to_all | solution.py:260
  28.9 1.6 slab_sum.2
  30.5 0.7 slice.24
  31.2 0.7 broadcast_in_dim.14
  31.9 4.6 %all-to-all-start.1 = ((f32[16,16,256]{2,1,0:T(8,128)}), f32[16,16,256]{2,1,0:T(8,128)S(1)}, u32[]{:S(2)}, u32[]{:S(2)}) async-start(f32[16,16,256]{2,1,0:T(8,128)} %broadcast_in_dim.14), calls=%async_computation.1 | async-start | bytes 524288 | tf_op jit(solution)/shard_map/all_to_all | solution.py:260
  36.6 1.3 slice.25.norms_ref
  37.9 9.9 %all-to-all-done.1.cross_ref = f32[16,16,256]{2,1,0:T(8,128)S(1)} async-done(((f32[16,16,256]{2,1,0:T(8,128)}), f32[16,16,256]{2,1,0:T(8,128)S(1)}, u32[]{:S(2)}, u32[]{:S(2)}) %all-to-all-start.1) | async-done | bytes 262176 | tf_op jit(solution)/shard_map/all_to_all | solution.py:260
  47.8 0.0 copy-start.2
  47.8 0.7 copy-done.2
  48.5 6.9 %cayley_one.1 = (bf16[512,512]{1,0:T(8,128)(2,1)}, bf16[512,512]{1,0:T(8,128)(2,1)}) custom-call(s32[1]{0:T(128)} %bitcast.1.swap_ref, f32[16,16,256]{2,1,0:T(8,128)} %copy-done.2, f32[8,256]{1,0:T(8,128)} %slice.25.norms_ref), custom_call_target="tpu_custom_call" | custom-call | tf_op jit(solution)/shard_map/cayley_one/pallas_call | solution.py:163
  55.4 9.0 %rotate.1 = (f32[2048,256]{1,0:T(8,128)}, f32[2048,256]{1,0:T(8,128)}) custom-call(f32[2048,512]{1,0:T(8,128)} %x_ref.1, bf16[512,512]{1,0:T(8,128)(2,1)} %get-tuple-element.15.high_ref, bf16[512,512]{1,0:T(8,128)(2,1)} %get-tuple-element.16.low_ref), custom_call_target="tpu_custom_call" | custom-call | tf_op jit(solution)/shard_map/rotate/pallas_call | solution.py:213
  64.3 0.7 collective-permute-start
  65.0 44.4 %collective-permute-done.left_ref = f32[2048,256]{1,0:T(8,128)S(1)} collective-permute-done((f32[2048,256]{1,0:T(8,128)}, f32[2048,256]{1,0:T(8,128)S(1)}, u32[]{:S(2)}, u32[]{:S(2)}) %collective-permute-start) | collective-permute-done | bytes 2097184 | tf_op jit(solution)/shard_map/ppermute | solution.py:282
  109.4 0.0 copy-start
  109.4 23.0 %collective-permute-start.1 = (f32[2048,256]{1,0:T(8,128)}, f32[2048,256]{1,0:T(8,128)}, u32[]{:S(2)}, u32[]{:S(2)}) collective-permute-start(f32[2048,256]{1,0:T(8,128)} %get-tuple-element.19.right_ref), channel_id=1, source_target_pairs={{2,0},{4,2},{6,4},{8,6},{10,8},{12,10},{14,12},{15,14},{13,15},{11... | collective-permute-start | bytes 6291464 | tf_op jit(solution)/shard_map/ppermute | solution.py:284
  132.4 0.0 copy-done
  132.4 4.7 %gram.3 = f32[16,40,128]{2,1,0:T(8,128)} custom-call(f32[2048,256]{1,0:T(8,128)} %copy-done, f32[2048,256]{1,0:T(8,128)} %get-tuple-element.19.right_ref), custom_call_target="tpu_custom_call" | custom-call | tf_op jit(solution)/shard_map/gram/pallas_call | solution.py:61
  137.0 18.0 %all_to_all.21.in_ref = f32[16,40,128]{2,1,0:T(8,128)} all-to-all(f32[16,40,128]{2,1,0:T(8,128)} %gram.3), channel_id=1, replica_groups=mesh['rows'=16,'pairs'=16] {'rows'}, dimensions={0} | all-to-all | bytes 655360 | tf_op jit(solution)/shard_map/all_to_all | solution.py:260
  155.0 1.6 slab_sum.3
  156.6 4.6 %collective-permute-start.2 = (f32[24,256]{1,0:T(8,128)}, f32[24,256]{1,0:T(8,128)S(1)}, u32[]{:S(2)}, u32[]{:S(2)}) collective-permute-start(f32[24,256]{1,0:T(8,128)} %slab_sum.3), channel_id=1, source_target_pairs={{2,0},{4,2},{6,4},{8,6},{10,8},{12,10},{14,12},{15,14},{13,15},{11... | collective-permute-start | bytes 73736 | tf_op jit(solution)/shard_map/ppermute | solution.py:287
  161.2 0.8 slice.26
  162.0 4.0 %collective-permute-done.2 = f32[24,256]{1,0:T(8,128)S(1)} collective-permute-done((f32[24,256]{1,0:T(8,128)}, f32[24,256]{1,0:T(8,128)S(1)}, u32[]{:S(2)}, u32[]{:S(2)}) %collective-permute-start.2) | collective-permute-done | bytes 24608 | tf_op jit(solution)/shard_map/ppermute | solution.py:287
  166.0 0.8 broadcast_in_dim.15
  166.9 8.5 %all-to-all-start.3 = ((f32[16,32,256]{2,1,0:T(8,128)}), f32[16,32,256]{2,1,0:T(8,128)S(1)}, u32[]{:S(2)}, u32[]{:S(2)}) async-start(f32[16,32,256]{2,1,0:T(8,128)} %broadcast_in_dim.15), calls=%async_computation.3 | async-start | bytes 1048576 | tf_op jit(solution)/shard_map/all_to_all | solution.py:260
  175.4 0.7 add_convert_fusion.marks_ref
  176.1 1.3 slice.28.norms_ref
  177.4 0.6 slice.29.other_ref
  178.0 12.5 %all-to-all-done.3.cross_ref = f32[16,32,256]{2,1,0:T(8,128)S(1)} async-done(((f32[16,32,256]{2,1,0:T(8,128)}), f32[16,32,256]{2,1,0:T(8,128)S(1)}, u32[]{:S(2)}, u32[]{:S(2)}) %all-to-all-start.3) | async-done | bytes 524320 | tf_op jit(solution)/shard_map/all_to_all | solution.py:260
  190.5 0.0 copy-start.1
  190.5 0.8 copy-done.1
  191.3 17.3 %cayley_two.1 = (bf16[512,256]{1,0:T(8,128)(2,1)}, bf16[512,256]{1,0:T(8,128)(2,1)}, bf16[512,256]{1,0:T(8,128)(2,1)}, bf16[512,256]{1,0:T(8,128)(2,1)}) custom-call(s32[4]{0:T(128)} %add_convert_fusion.marks_ref, f32[16,32,256]{2,1,0:T(8,128)} %copy-done.1, f32[8,256]{1,0:T(8,128)} %slice.28.norms_ref, f32[8,256]{1,0:T(8,128)} %slice.29.other_ref), custom_call_target="tpu_custom_call" | custom-call | tf_op jit(solution)/shard_map/cayley_two/pallas_call | solution.py:190
  208.7 7.5 %combine.2.refs_0_ = f32[2048,512]{1,0:T(8,128)} custom-call(s32[1]{0:T(128)} %bitcast.at_ref, f32[2048,256]{1,0:T(8,128)} %copy-done, f32[2048,256]{1,0:T(8,128)} %get-tuple-element.19.right_ref, bf16[512,256]{1,0:T(8,128)(2,1)} %get-tuple-element.23.high_ref, bf16[512,256]{1,0:T(8,128)(2,1)} %get-tuple-element.24.low_ref), custom_call_target="tpu_custom_call" | custom-call | tf_op jit(solution)/shard_map/combine/pallas_call | solution.py:245
  216.2 0.0 collective-permute-done.1.right_ref
  216.2 7.5 %combine.3 = f32[2048,512]{1,0:T(8,128)} custom-call(s32[1]{0:T(128)S(6)} %sub.3.at_ref, f32[2048,256]{1,0:T(8,128)} %get-tuple-element.17.left_ref, f32[2048,256]{1,0:T(8,128)} %collective-permute-done.1.right_ref, bf16[512,256]{1,0:T(8,128)(2,1)} %get-tuple-element.21.high_ref, ...), custom_call_target="tpu_custom_call", output_to_operand_aliasing={{}: (5, {})} | custom-call | tf_op jit(solution)/shard_map/combine/pallas_call | solution.py:245
  (2 shorter events, 0.0 us)
Async XLA Ops:
  31.9 15.8 %all-to-all-start.1 = ((f32[16,16,256]{2,1,0:T(8,128)}), f32[16,16,256]{2,1,0:T(8,128)S(1)}, u32[]{:S(2)}, u32[]{:S(2)}) async-start(f32[16,16,256]{2,1,0:T(8,128)} %broadcast_in_dim.14), calls=%async_computation.1 | async-start | bytes 524288 | tf_op jit(solution)/shard_map/all_to_all | solution.py:260
  47.8 0.7 copy-start.2
  64.3 45.1 %collective-permute-start = (f32[2048,256]{1,0:T(8,128)}, f32[2048,256]{1,0:T(8,128)S(1)}, u32[]{:S(2)}, u32[]{:S(2)}) collective-permute-start(f32[2048,256]{1,0:T(8,128)} %get-tuple-element.17.left_ref), channel_id=1, source_target_pairs={{0,2},{2,4},{4,6},{6,8},{8,10},{10,12},{12,14},{14,15},{15,13},{13... | collective-permute-start | bytes 6291464 | tf_op jit(solution)/shard_map/ppermute | solution.py:282
  109.4 23.0 %copy-start = (f32[2048,256]{1,0:T(8,128)}, f32[2048,256]{1,0:T(8,128)S(1)}, u32[]{:S(2)}) copy-start(f32[2048,256]{1,0:T(8,128)S(1)} %collective-permute-done.left_ref) | copy-start | bytes 6291460
  109.4 106.7 %collective-permute-start.1 = (f32[2048,256]{1,0:T(8,128)}, f32[2048,256]{1,0:T(8,128)}, u32[]{:S(2)}, u32[]{:S(2)}) collective-permute-start(f32[2048,256]{1,0:T(8,128)} %get-tuple-element.19.right_ref), channel_id=1, source_target_pairs={{2,0},{4,2},{6,4},{8,6},{10,8},{12,10},{14,12},{15,14},{13,15},{11... | collective-permute-start | bytes 6291464 | tf_op jit(solution)/shard_map/ppermute | solution.py:284
  156.6 9.4 %collective-permute-start.2 = (f32[24,256]{1,0:T(8,128)}, f32[24,256]{1,0:T(8,128)S(1)}, u32[]{:S(2)}, u32[]{:S(2)}) collective-permute-start(f32[24,256]{1,0:T(8,128)} %slab_sum.3), channel_id=1, source_target_pairs={{2,0},{4,2},{6,4},{8,6},{10,8},{12,10},{14,12},{15,14},{13,15},{11... | collective-permute-start | bytes 73736 | tf_op jit(solution)/shard_map/ppermute | solution.py:287
  166.9 23.7 %all-to-all-start.3 = ((f32[16,32,256]{2,1,0:T(8,128)}), f32[16,32,256]{2,1,0:T(8,128)S(1)}, u32[]{:S(2)}, u32[]{:S(2)}) async-start(f32[16,32,256]{2,1,0:T(8,128)} %broadcast_in_dim.15), calls=%async_computation.3 | async-start | bytes 1048576 | tf_op jit(solution)/shard_map/all_to_all | solution.py:260
  190.5 0.8 copy-start.1

commit v2 on v1

v2 whole, which is shorter than its diff:
```python
import jax
import jax.numpy as jnp
from jax import lax
from jax.experimental import pallas as pl
from jax.experimental.pallas import tpu as pltpu
from jax.sharding import PartitionSpec as P


F32, BF16 = jnp.float32, jnp.bfloat16
TAIL = 8
LANES = 128


def halves(x):
    high = x.astype(BF16)
    return high, (x - high.astype(F32)).astype(BF16)


def product(a, b, dims=((1,), (0,))):
    return lax.dot_general(a, b, (dims, ((), ())), preferred_element_type=F32)


def three_products(a, b, dims=((1,), (0,))):
    (a_high, a_low), (b_high, b_low) = halves(a), halves(b)
    return product(a_high, b_high, dims) + (product(a_high, b_low, dims) + product(a_low, b_high, dims))


def full_product(a, b, dims=((1,), (0,))):
    return lax.dot_general(
        a, b, (dims, ((), ())), precision=lax.Precision.HIGHEST, preferred_element_type=F32
    )


def gram_parts(lefts, rights, cols, before=()):
    pieces = len(lefts)

    def kernel(*refs):
        ins, (acc_ref, norms_ref) = refs[:-2], refs[-2:]
        acc = norms = None
        for a_ref, b_ref in zip(ins[:pieces], ins[pieces : 2 * pieces]):
            a, b = a_ref[...], b_ref[...]
            part = three_products(a, b, ((0,), (0,)))
            squares = jnp.concatenate([a * a, b * b], axis=1)
            squares = jnp.sum(squares.reshape(a.shape[0] // 8, 8, 2 * cols), axis=0)
            acc = part if acc is None else acc + part
            norms = squares if norms is None else norms + squares
        if before:
            acc, norms = acc + ins[-2][...], norms + ins[-1][...]
        acc_ref[...] = acc
        norms_ref[...] = norms

    return pl.pallas_call(
        kernel,
        out_shape=(
            jax.ShapeDtypeStruct((cols, cols), F32),
            jax.ShapeDtypeStruct((8, 2 * cols), F32),
        ),
        name="gram_parts",
    )(*lefts, *rights, *before)


def store_slabs(out_ref, acc_ref, norms, peers, cols):
    per, wide = cols // peers, cols // LANES
    total = jnp.sum(norms, axis=0, keepdims=True)
    lines = [total[:, LANES * q : LANES * (q + 1)] for q in range(2 * wide)]
    tail = jnp.concatenate([*lines, jnp.zeros((TAIL - 2 * wide, LANES), F32)], axis=0)
    for peer in range(peers):
        rows = acc_ref[peer * per : (peer + 1) * per, :]
        for q in range(wide):
            out_ref[peer, q * per : (q + 1) * per, :] = rows[:, LANES * q : LANES * (q + 1)]
        out_ref[peer, wide * per :, :] = tail


def gram(left, left_at, right, right_at, rows, peers, cols, before=(), block=512):
    per, wide = cols // peers, cols // LANES

    def kernel(left_ref, right_ref, *refs):
        out_ref, acc_ref, norms_ref = refs[-3:]
        step = pl.program_id(0)

        @pl.when(step == 0)
        def _():
            if before:
                acc_ref[...] = refs[0][...]
                norms_ref[...] = refs[1][...]
            else:
                acc_ref[...] = jnp.zeros_like(acc_ref)
                norms_ref[...] = jnp.zeros_like(norms_ref)

        a, b = left_ref[...], right_ref[...]
        acc_ref[...] += three_products(a, b, ((0,), (0,)))
        norms_ref[:, :cols] += jnp.sum((a * a).reshape(block // 8, 8, cols), axis=0)
        norms_ref[:, cols:] += jnp.sum((b * b).reshape(block // 8, 8, cols), axis=0)

        @pl.when(step == pl.num_programs(0) - 1)
        def _():
            store_slabs(out_ref, acc_ref, norms_ref[...], peers, cols)

    shape = (peers, wide * per + TAIL, LANES)
    return pl.pallas_call(
        kernel,
        grid=(rows // block,),
        in_specs=[
            pl.BlockSpec((block, cols), lambda i: (i, left_at)),
            pl.BlockSpec((block, cols), lambda i: (i, right_at)),
            *[pl.BlockSpec(x.shape, lambda i: (0, 0)) for x in before],
        ],
        out_specs=pl.BlockSpec(shape, lambda i: (0, 0, 0)),
        out_shape=jax.ShapeDtypeStruct(shape, F32),
        scratch_shapes=[pltpu.VMEM((cols, cols), F32), pltpu.VMEM((8, 2 * cols), F32)],
        name="gram",
    )(left, right, *before)


def slab_sum(slabs, cols, spread):
    peers = slabs.shape[0]
    per, wide = cols // peers, cols // LANES

    def kernel(in_ref, out_ref, norms_ref):
        total = in_ref[0]
        for peer in range(1, peers):
            total = total + in_ref[peer]
        rows = jnp.concatenate([total[q * per : (q + 1) * per] for q in range(wide)], axis=1)
        if spread:
            for peer in range(peers):
                out_ref[peer] = rows
        else:
            out_ref[:per] = rows
        tail = total[wide * per :]
        norms = []
        for side in range(2):
            lines = [tail[side * wide + q : side * wide + q + 1] for q in range(wide)]
            norms.append(jnp.concatenate(lines, axis=1))
        norms = jnp.concatenate([*norms, jnp.zeros((TAIL - 2, cols), F32)], axis=0)
        norms_ref[...] = norms
        if not spread:
            out_ref[per:] = norms

    shape = (peers, per, cols) if spread else (per + TAIL, cols)
    return pl.pallas_call(
        kernel,
        out_shape=(jax.ShapeDtypeStruct(shape, F32), jax.ShapeDtypeStruct((TAIL, cols), F32)),
        name="slab_sum",
    )(slabs)


def paired(mine, other, partner, peers, per):
    cols = mine.shape[1]

    def kernel(mine_ref, other_ref, partner_ref, out_ref, norms_ref, other_norms_ref):
        sums = []
        for edge, ref in enumerate((mine_ref, other_ref)):
            begin = edge * (per + TAIL)
            sums.append(ref[...] + partner_ref[begin : begin + per + TAIL])
        for peer in range(peers):
            out_ref[peer, :per] = sums[0][:per]
            out_ref[peer, per:] = sums[1][:per]
        norms_ref[...] = sums[0][per:]
        other_norms_ref[...] = sums[1][per:]

    norms = jax.ShapeDtypeStruct((TAIL, cols), F32)
    return pl.pallas_call(
        kernel,
        out_shape=(jax.ShapeDtypeStruct((peers, 2 * per, cols), F32), norms, norms),
        name="paired",
    )(mine, other, partner)


def cayley(edges, rows_all, power_refs, inverse_refs):
    cols = edges[0][0].shape[0]
    row_at = lax.broadcasted_iota(jnp.int32, (cols, cols), 0)
    col_at = lax.broadcasted_iota(jnp.int32, (cols, cols), 1)
    diagonal = row_at == col_at
    identity = jnp.where(diagonal, 1.0, 0.0).astype(F32)
    couplings, systems, bounds = [], [], []
    for cross, norms, sign in edges:
        scale_left = lax.rsqrt(norms[0:1] / rows_all + 1e-06)
        scale_right = lax.rsqrt(norms[1:2] / rows_all + 1e-06)
        spread = jnp.where(diagonal, jnp.broadcast_to(scale_left, (cols, cols)), 0.0)
        scale_left = jnp.sum(spread, axis=1, keepdims=True)
        coupling = (0.5 * sign) * cross * scale_left * scale_right / rows_all
        couplings.append(coupling)
        systems.append(identity + full_product(coupling, coupling, ((1,), (1,))))
    for system, power_ref, inverse_ref in zip(systems, power_refs, inverse_refs):
        bound = jnp.max(jnp.sum(jnp.abs(system), axis=0, keepdims=True))
        factor = 2.0 / (1.0 + bound)
        power = identity - factor * system
        inverse_ref[...] = factor * (identity + power)
        power_ref[...] = power
        bounds.append(bound)
    largest = bounds[0] if len(bounds) == 1 else jnp.maximum(*bounds)
    ratio = (largest - 1.0) / (largest + 1.0)

    def more(carry):
        left, count = carry
        return (left > 1e-3) & (count < 40)

    def double(carry):
        left, count = carry
        squares = []
        for power_ref in power_refs:
            before = power_ref[...]
            squares.append(three_products(before, before))
        for squared, power_ref, inverse_ref in zip(squares, power_refs, inverse_refs):
            power_ref[...] = squared
            inverse = inverse_ref[...]
            inverse_ref[...] = inverse + three_products(inverse, squared)
        return left * left, count + 1

    lax.while_loop(more, double, (ratio * ratio, jnp.int32(0)))

    def newton(_, carry):
        gaps = [identity - full_product(s, ref[...]) for s, ref in zip(systems, inverse_refs)]
        for gap, inverse_ref in zip(gaps, inverse_refs):
            inverse = inverse_ref[...]
            inverse_ref[...] = inverse + full_product(inverse, gap)
        return carry

    lax.fori_loop(0, jnp.where(largest < 8.0, 1, 3), newton, 0)
    inverses = [ref[...] for ref in inverse_refs]
    uppers = [full_product(x, e) for x, e in zip(inverses, couplings)]
    lowers = [full_product(e, y, ((0,), (0,))) for e, y in zip(couplings, uppers)]
    return [
        (2.0 * x - identity, 2.0 * y, -2.0 * y.T, identity - 2.0 * z)
        for x, y, z in zip(inverses, uppers, lowers)
    ]


def store_halves(high_ref, low_ref, at_row, at_col, value):
    rows, cols = value.shape
    high, low = halves(value)
    high_ref[at_row : at_row + rows, at_col : at_col + cols] = high
    low_ref[at_row : at_row + rows, at_col : at_col + cols] = low


def step_one_matrices(gathered, norms, swap, rows_all):
    cols = gathered.shape[2]

    def kernel(swap_ref, cross_ref, norms_ref, high_ref, low_ref, power_ref, inverse_ref):
        cross = cross_ref[...].reshape(cols, cols)
        edge = (cross, norms_ref[...], 1.0)
        blocks = cayley([edge], rows_all, [power_ref], [inverse_ref])[0]
        turned = swap_ref[0] != 0
        for line in range(2):
            near, far = blocks[2 * line], blocks[2 * line + 1]
            store_halves(high_ref, low_ref, line * cols, 0, jnp.where(turned, far, near))
            store_halves(high_ref, low_ref, line * cols, cols, jnp.where(turned, near, far))

    out = jax.ShapeDtypeStruct((2 * cols, 2 * cols), BF16)
    vmem = pl.BlockSpec(memory_space=pltpu.VMEM)
    return pl.pallas_call(
        kernel,
        in_specs=[pl.BlockSpec(memory_space=pltpu.SMEM), vmem, vmem],
        out_shape=(out, out),
        scratch_shapes=[pltpu.VMEM((cols, cols), F32)] * 2,
        name="cayley_one",
    )(swap, gathered, norms)


def step_two_matrices(gathered, norms, other_norms, marks, rows_all):
    _, both, cols = gathered.shape
    per = both // 2

    def kernel(marks_ref, cross_ref, norms_ref, other_ref, *refs):
        outs, power_refs, inverse_refs = refs[:4], refs[4:6], refs[6:]
        edges = []
        for edge in range(2):
            cross = cross_ref[:, edge * per : (edge + 1) * per, :].reshape(cols, cols)
            sign = jnp.where(marks_ref[2 * edge] != 0, 1.0, -1.0).astype(F32)
            edges.append((cross, (norms_ref, other_ref)[edge][...], sign))
        for edge, blocks in enumerate(cayley(edges, rows_all, power_refs, inverse_refs)):
            moved_role = marks_ref[2 * edge + 1] != 0
            for line in range(2):
                value = jnp.where(moved_role, blocks[2 * line], blocks[2 * line + 1])
                store_halves(outs[2 * edge], outs[2 * edge + 1], line * cols, 0, value)

    out = jax.ShapeDtypeStruct((2 * cols, cols), BF16)
    vmem = pl.BlockSpec(memory_space=pltpu.VMEM)
    return pl.pallas_call(
        kernel,
        in_specs=[pl.BlockSpec(memory_space=pltpu.SMEM), vmem, vmem, vmem],
        out_shape=(out,) * 4,
        scratch_shapes=[pltpu.VMEM((cols, cols), F32)] * 4,
        name="cayley_two",
    )(marks, gathered, norms, other_norms)


def rotate(both, high, low, part, start, rows, block=512):
    width = both.shape[1]
    cols = width // 2

    def kernel(x_ref, high_ref, low_ref, out_ref):
        x_high, x_low = halves(x_ref[...])
        out_ref[...] = product(x_high, high_ref[...]) + (
            product(x_high, low_ref[...]) + product(x_low, high_ref[...])
        )

    at = start // block
    fixed = pl.BlockSpec((width, cols), lambda i: (0, part))
    return pl.pallas_call(
        kernel,
        grid=(rows // block,),
        in_specs=[pl.BlockSpec((block, width), lambda i: (i + at, 0)), fixed, fixed],
        out_specs=pl.BlockSpec((block, cols), lambda i: (i, 0)),
        out_shape=jax.ShapeDtypeStruct((rows, cols), F32),
        name="rotate",
    )(both, high, low)


def combine(at, lefts, rights, high, low, start, rows, before=None, block=512):
    cols = lefts[0].shape[1]
    steps = [x.shape[0] // block for x in lefts]
    begins = [sum(steps[:k]) for k in range(len(steps))]
    pieces, first = len(steps), start // block

    def kernel(at_ref, *refs):
        high_ref, low_ref, out_ref = refs[2 * pieces], refs[2 * pieces + 1], refs[-1]
        step = pl.program_id(0)
        for k in range(pieces):

            @pl.when((step >= begins[k]) & (step < begins[k] + steps[k]))
            def _(k=k):
                total = None
                for line, ref in enumerate((refs[k], refs[pieces + k])):
                    x_high, x_low = halves(ref[...])
                    m_high = high_ref[line * cols : (line + 1) * cols, :]
                    m_low = low_ref[line * cols : (line + 1) * cols, :]
                    part = product(x_high, m_high) + (
                        product(x_high, m_low) + product(x_low, m_high)
                    )
                    total = part if total is None else total + part
                out_ref[...] = total

    data = [
        pl.BlockSpec((block, cols), lambda i, at_ref, b=b, n=n: (jnp.clip(i - b, 0, n - 1), 0))
        for b, n in zip(begins, steps)
    ]
    fixed = pl.BlockSpec((2 * cols, cols), lambda i, at_ref: (0, 0))
    operands = [at, *lefts, *rights, high, low]
    in_specs = [*data, *data, fixed, fixed]
    aliases = {}
    if before is not None:
        operands.append(before)
        in_specs.append(pl.BlockSpec(memory_space=pl.ANY))
        aliases = {len(operands) - 1: 0}
    return pl.pallas_call(
        kernel,
        grid_spec=pltpu.PrefetchScalarGridSpec(
            num_scalar_prefetch=1,
            grid=(sum(steps),),
            in_specs=in_specs,
            out_specs=pl.BlockSpec((block, cols), lambda i, at_ref: (i + first, at_ref[0])),
        ),
        out_shape=jax.ShapeDtypeStruct((rows, 2 * cols), F32),
        input_output_aliases=aliases,
        name="combine",
    )(*operands)


def exchanged(blocks, groups=None):
    return lax.all_to_all(blocks, "rows", 0, 0, axis_index_groups=groups, tiled=True)


def held(value, *until):
    return lax.optimization_barrier((value, *until))[0]


def shards(matrix):
    cols = matrix.shape[1] // 2
    rows = matrix.shape[0]
    peers = lax.axis_size("rows")
    rows_all = rows * peers
    per = cols // peers
    position = lax.axis_index("pairs")
    size = lax.axis_size("pairs")
    ring = [*range(0, size, 2), *range(size - 1, 0, -2)]
    clockwise = [(ring[i], ring[(i + 1) % size]) for i in range(size)]
    back = [(b, a) for a, b in clockwise]
    even = position % 2 == 0
    pieces = [(0, rows // 2), (rows // 2, rows // 4), (3 * rows // 4, rows // 4)]

    slabs = exchanged(gram(matrix, 0, matrix, 1, rows, peers, cols, block=rows // 2))
    spread, norms = slab_sum(slabs, cols, True)
    gathered = exchanged(spread)
    swap = jnp.where(even & (position > 0), 0, 1).astype(jnp.int32)[None]
    high, low = step_one_matrices(gathered, norms, swap, float(rows_all))
    onward, arrived = [], []
    for k, piece in enumerate(pieces):
        onward.append(rotate(matrix, high, low, 0, *piece))
        arrived.append(lax.ppermute(onward[k], "pairs", clockwise))
    kept = [rotate(matrix, high, low, 1, *piece) for piece in pieces]

    line = peers // 2
    halves_of_rows = [[*range(line)], [*range(line, peers)]]
    across = [(i, (i + line) % peers) for i in range(peers)]
    per = cols // line
    begun = ()
    for k in range(2):
        begun = gram_parts(arrived[k : k + 1], kept[k : k + 1], cols, begun)
    slabs = gram(arrived[2], 0, kept[2], 0, pieces[2][1], line, cols, begun)
    returned = [None] * 3
    returned[1] = lax.ppermute(held(kept[1], slabs), "pairs", back)
    slabs = exchanged(slabs, halves_of_rows)
    mine, _ = slab_sum(slabs, cols, False)
    other = lax.ppermute(mine, "pairs", back)
    partner = lax.ppermute(jnp.concatenate([mine, other], axis=0), "rows", across)
    for at in (0, 2):
        returned[at] = lax.ppermute(held(kept[at], partner), "pairs", back)
    pair, norms, other_norms = paired(mine, other, partner, line, per)
    gathered = exchanged(pair, halves_of_rows)
    marks = jnp.stack(
        [
            (even & (position > 0)) | (position == size - 1),
            position != 0,
            even,
            position == 1,
        ]
    ).astype(jnp.int32)
    matrices = step_two_matrices(gathered, norms, other_norms, marks, float(rows_all))
    in_first = jnp.where(even, 0, 1).astype(jnp.int32)[None]
    done = combine(in_first, arrived, kept, *matrices[:2], 0, rows)
    for k in (slice(0, 2), slice(2, 3)):
        done = combine(
            1 - in_first, onward[k], returned[k], *matrices[2:], pieces[k.start][0], rows, done
        )
    return done


def solution(mesh):
    return jax.shard_map(
        shards,
        mesh=mesh,
        in_specs=(P("rows", "pairs"),),
        out_specs=P("rows", "pairs"),
        check_vma=False,
    )
```

time: 225 us -> 186 us (0.83)
  the two profiles are of different devices: /device:TPU:2 before, /device:TPU:4 now
where the time goes in v2:
time: 186 us; the launch traced here: 185 us
  Pallas kernels  65.1 us (35%)
  waiting for transfers between devices  56 us (30%)
  blocking collectives  43.4 us (23%)
  starting transfers between devices  16 us (9%)
  local copies, waits for them, and re-layouts  3.31 us (2%)
    all_to_all x2, blocking collectives, exchanged(): lax.all_to_all(blocks, 'rows', 0, 0, axis_index_groups=groups, tiled=True)  43.4 us
    all_to_all x2, waiting for transfers between devices, exchanged(): lax.all_to_all(blocks, 'rows', 0, 0, axis_index_groups=groups, tiled=True)  23.9 us
    ppermute x3, waiting for transfers between devices, shards(): arrived.append(lax.ppermute(onward[k], 'pairs', clockwise))  20.4 us
    pallas_call x6, Pallas kernels, rotate(): pl.pallas_call(kernel, grid=(rows // block,), in_specs=[pl.BlockSpec((blo...  17.5 us
    pallas_call x3, Pallas kernels, combine(): pl.pallas_call(kernel, grid_spec=pltpu.PrefetchScalarGridSpec(num_scalar_...  12.7 us
    pallas_call x1, Pallas kernels, step_two_matrices(): pl.pallas_call(kernel, in_specs=[pl.BlockSpec(memory_space=pltpu.SMEM), v...  11.1 us
    all_to_all x2, starting transfers between devices, exchanged(): lax.all_to_all(blocks, 'rows', 0, 0, axis_index_groups=groups, tiled=True)  8.11 us
    pallas_call x1, Pallas kernels, step_one_matrices(): pl.pallas_call(kernel, in_specs=[pl.BlockSpec(memory_space=pltpu.SMEM), v...  6.91 us
  transfers between devices with their start and end apart: 10, of which 9 were waited for; matrix products, arithmetic and copies ran while one was open for 0% of the time, Pallas kernels for 23%

profile of v2, /device:TPU:4, one launch (start us, length us, event | category | flops | bytes accessed | tf_op | source)
XLA Modules:
  0.0 185.4 jit_solution(2838457427516226961)
XLA Ops:
  0.0 3.8 %gram.2 = f32[16,40,128]{2,1,0:T(8,128)} custom-call(f32[2048,512]{1,0:T(8,128)} %x_ref.11, f32[2048,512]{1,0:T(8,128)} %x_ref.11), custom_call_target="tpu_custom_call" | custom-call | tf_op jit(solution)/shard_map/gram/pallas_call | solution.py:100
  3.8 24.2 %all_to_all.20.in_ref = f32[16,40,128]{2,1,0:T(8,128)} all-to-all(f32[16,40,128]{2,1,0:T(8,128)} %gram.2), channel_id=1, replica_groups=mesh['rows'=16,'pairs'=16] {'rows'}, dimensions={0} | all-to-all | bytes 655360 | tf_op jit(solution)/shard_map/all_to_all | solution.py:361
  28.1 1.7 slab_sum.2
  29.8 4.6 %all-to-all-start.1 = ((f32[16,16,256]{2,1,0:T(8,128)}), f32[16,16,256]{2,1,0:T(8,128)S(1)}, u32[]{:S(2)}, u32[]{:S(2)}) async-start(f32[16,16,256]{2,1,0:T(8,128)} %get-tuple-element.24), calls=%async_computation.1 | async-start | bytes 524288 | tf_op jit(solution)/shard_map/all_to_all | solution.py:361
  34.4 11.2 %all-to-all-done.1.cross_ref = f32[16,16,256]{2,1,0:T(8,128)S(1)} async-done(((f32[16,16,256]{2,1,0:T(8,128)}), f32[16,16,256]{2,1,0:T(8,128)S(1)}, u32[]{:S(2)}, u32[]{:S(2)}) %all-to-all-start.1) | async-done | bytes 262176 | tf_op jit(solution)/shard_map/all_to_all | solution.py:361
  45.6 0.7 copy-done.5
  46.3 6.9 %cayley_one.1 = (bf16[512,512]{1,0:T(8,128)(2,1)}, bf16[512,512]{1,0:T(8,128)(2,1)}) custom-call(s32[1]{0:T(128)} %bitcast.1.swap_ref, f32[16,16,256]{2,1,0:T(8,128)} %copy-done.5, f32[8,256]{1,0:T(8,128)} %get-tuple-element.25.norms_ref), custom_call_target="tpu_custom_call" | custom-call | tf_op jit(solution)/shard_map/cayley_one/pallas_call | solution.py:251
  53.2 3.3 %rotate.10.refs_0_ = f32[1024,256]{1,0:T(8,128)} custom-call(f32[2048,512]{1,0:T(8,128)} %x_ref.11, bf16[512,512]{1,0:T(8,128)(2,1)} %get-tuple-element.26.high_ref, bf16[512,512]{1,0:T(8,128)(2,1)} %get-tuple-element.27.low_ref), custom_call_target="tpu_custom_call" | custom-call | tf_op jit(solution)/shard_map/rotate/pallas_call | solution.py:300
  56.5 0.7 collective-permute-start.2
  57.2 2.7 %rotate.8.refs_1_ = f32[512,256]{1,0:T(8,128)} custom-call(f32[2048,512]{1,0:T(8,128)} %x_ref.11, bf16[512,512]{1,0:T(8,128)(2,1)} %get-tuple-element.26.high_ref, bf16[512,512]{1,0:T(8,128)(2,1)} %get-tuple-element.27.low_ref), custom_call_target="tpu_custom_call" | custom-call | tf_op jit(solution)/shard_map/rotate/pallas_call | solution.py:300
  59.9 2.0 %collective-permute-start.1 = (f32[512,256]{1,0:T(8,128)}, f32[512,256]{1,0:T(8,128)}, u32[]{:S(2)}, u32[]{:S(2)}) collective-permute-start(f32[512,256]{1,0:T(8,128)} %rotate.8.refs_1_), channel_id=1, source_target_pairs={{0,2},{2,4},{4,6},{6,8},{8,10},{10,12},{12,14},{14,15},{15,13},{13... | collective-permute-start | bytes 1572872 | tf_op jit(solution)/shard_map/ppermute | solution.py:390
  61.9 2.7 %rotate.6.refs_0_ = f32[512,256]{1,0:T(8,128)} custom-call(f32[2048,512]{1,0:T(8,128)} %x_ref.11, bf16[512,512]{1,0:T(8,128)(2,1)} %get-tuple-element.26.high_ref, bf16[512,512]{1,0:T(8,128)(2,1)} %get-tuple-element.27.low_ref), custom_call_target="tpu_custom_call" | custom-call | tf_op jit(solution)/shard_map/rotate/pallas_call | solution.py:300
  64.6 0.7 collective-permute-start
  65.3 3.3 %rotate.11.refs_1_.refs_3_ = f32[1024,256]{1,0:T(8,128)} custom-call(f32[2048,512]{1,0:T(8,128)} %x_ref.11, bf16[512,512]{1,0:T(8,128)(2,1)} %get-tuple-element.26.high_ref, bf16[512,512]{1,0:T(8,128)(2,1)} %get-tuple-element.27.low_ref), custom_call_target="tpu_custom_call" | custom-call | tf_op jit(solution)/shard_map/rotate/pallas_call | solution.py:300
  68.6 2.7 %rotate.9.refs_1_.refs_4_ = f32[512,256]{1,0:T(8,128)} custom-call(f32[2048,512]{1,0:T(8,128)} %x_ref.11, bf16[512,512]{1,0:T(8,128)(2,1)} %get-tuple-element.26.high_ref, bf16[512,512]{1,0:T(8,128)(2,1)} %get-tuple-element.27.low_ref), custom_call_target="tpu_custom_call" | custom-call | tf_op jit(solution)/shard_map/rotate/pallas_call | solution.py:300
  71.4 2.7 %rotate.7.right_ref.refs_5_ = f32[512,256]{1,0:T(8,128)} custom-call(f32[2048,512]{1,0:T(8,128)} %x_ref.11, bf16[512,512]{1,0:T(8,128)(2,1)} %get-tuple-element.26.high_ref, bf16[512,512]{1,0:T(8,128)(2,1)} %get-tuple-element.27.low_ref), custom_call_target="tpu_custom_call" | custom-call | tf_op jit(solution)/shard_map/rotate/pallas_call | solution.py:300
  74.1 15.6 %collective-permute-done.2.refs_0_ = f32[1024,256]{1,0:T(8,128)S(1)} collective-permute-done((f32[1024,256]{1,0:T(8,128)}, f32[1024,256]{1,0:T(8,128)S(1)}, u32[]{:S(2)}, u32[]{:S(2)}) %collective-permute-start.2) | collective-permute-done | bytes 1048608 | tf_op jit(solution)/shard_map/ppermute | solution.py:390
  89.7 1.0 copy-done.3
  90.7 3.0 %gram_parts.2 = (f32[256,256]{1,0:T(8,128)}, f32[8,512]{1,0:T(8,128)}) custom-call(f32[1024,256]{1,0:T(8,128)} %copy-done.3, f32[1024,256]{1,0:T(8,128)} %rotate.11.refs_1_.refs_3_), custom_call_target="tpu_custom_call" | custom-call | tf_op jit(solution)/shard_map/gram_parts/pallas_call | solution.py:52
  93.7 1.6 collective-permute-done.1.refs_0_.refs_1_
  95.3 2.5 %gram_parts.3 = (f32[256,256]{1,0:T(8,128)}, f32[8,512]{1,0:T(8,128)}) custom-call(f32[512,256]{1,0:T(8,128)} %collective-permute-done.1.refs_0_.refs_1_, f32[512,256]{1,0:T(8,128)} %rotate.9.refs_1_.refs_4_, f32[256,256]{1,0:T(8,128)} %get-tuple-element.28.refs_2_, f32[8,512]{1,0:T(8,128)} %get-tuple-element.29.refs_3_), custom_call_target="tpu_custom_call" | custom-call | tf_op jit(solution)/shard_map/gram_parts/pallas_call | solution.py:52
  97.8 3.2 %collective-permute-done.left_ref.refs_2_ = f32[512,256]{1,0:T(8,128)} collective-permute-done((f32[512,256]{1,0:T(8,128)}, f32[512,256]{1,0:T(8,128)}, u32[]{:S(2)}, u32[]{:S(2)}) %collective-permute-start) | collective-permute-done | bytes 524320 | tf_op jit(solution)/shard_map/ppermute | solution.py:390
  101.0 2.4 %gram.3 = f32[8,72,128]{2,1,0:T(8,128)} custom-call(f32[512,256]{1,0:T(8,128)} %collective-permute-done.left_ref.refs_2_, f32[512,256]{1,0:T(8,128)} %rotate.7.right_ref.refs_5_, f32[256,256]{1,0:T(8,128)} %get-tuple-element.30.refs_0_, f32[8,512]{1,0:T(8,128)} %get-tuple-element.31.refs_1_), custom_call_target="tpu_custom_call" | custom-call | tf_op jit(solution)/shard_map/gram/pallas_call | solution.py:100
  103.4 19.2 %all_to_all.21.in_ref = f32[8,72,128]{2,1,0:T(8,128)} all-to-all(f32[8,72,128]{2,1,0:T(8,128)} %gram.3), channel_id=1, replica_groups={{0,16,32,48,64,80,96,112},{128,144,160,176,192,208,224,240},{1,17,33,49..., dimensions={0} | all-to-all | bytes 589824 | tf_op jit(solution)/shard_map/all_to_all | solution.py:361
  122.6 1.6 slab_sum.3
  124.2 0.0 collective-permute-start.3
  124.2 4.3 %collective-permute-done.3.other_ref = f32[40,256]{1,0:T(8,128)S(1)} collective-permute-done((f32[40,256]{1,0:T(8,128)}, f32[40,256]{1,0:T(8,128)S(1)}, u32[]{:S(2)}, u32[]{:S(2)}) %collective-permute-start.3) | collective-permute-done | bytes 40992 | tf_op jit(solution)/shard_map/ppermute | solution.py:405
  128.4 0.8 pad_maximum_fusion
  129.2 1.3 collective-permute-start.4
  130.6 4.7 %collective-permute-done.4.partner_ref = f32[80,256]{1,0:T(8,128)S(1)} collective-permute-done((f32[80,256]{1,0:T(8,128)S(1)}, f32[80,256]{1,0:T(8,128)S(1)}, u32[]{:S(2)}, u32[]{:S(2)}) %collective-permute-start.4) | collective-permute-done | bytes 81952 | tf_op jit(solution)/shard_map/ppermute | solution.py:406
  135.2 0.0 copy-done
  135.2 0.8 collective-permute-start.6
  136.1 0.0 copy-done.7
  136.1 1.8 paired.1
  137.8 3.5 %all-to-all-start.3 = ((f32[8,64,256]{2,1,0:T(8,128)}), f32[8,64,256]{2,1,0:T(8,128)S(1)}, u32[]{:S(2)}, u32[]{:S(2)}) async-start(f32[8,64,256]{2,1,0:T(8,128)} %get-tuple-element.34), calls=%async_computation.3 | async-start | bytes 1048576 | tf_op jit(solution)/shard_map/all_to_all | solution.py:361
  141.3 1.2 collective-permute-start.7
  142.6 1.2 collective-permute-start.5
  143.8 0.6 add_convert_fusion.marks_ref
  144.4 12.8 %all-to-all-done.3.cross_ref = f32[8,64,256]{2,1,0:T(8,128)S(1)} async-done(((f32[8,64,256]{2,1,0:T(8,128)}), f32[8,64,256]{2,1,0:T(8,128)S(1)}, u32[]{:S(2)}, u32[]{:S(2)}) %all-to-all-start.3) | async-done | bytes 524320 | tf_op jit(solution)/shard_map/all_to_all | solution.py:361
  157.2 0.8 copy-done.4
  158.0 11.1 %cayley_two.1 = (bf16[512,256]{1,0:T(8,128)(2,1)}, bf16[512,256]{1,0:T(8,128)(2,1)}, bf16[512,256]{1,0:T(8,128)(2,1)}, bf16[512,256]{1,0:T(8,128)(2,1)}) custom-call(s32[4]{0:T(128)} %add_convert_fusion.marks_ref, f32[8,64,256]{2,1,0:T(8,128)} %copy-done.4, f32[8,256]{1,0:T(8,128)} %get-tuple-element.35.norms_ref, f32[8,256]{1,0:T(8,128)} %get-tuple-element.36.other_ref), custom_call_target="tpu_custom_call" | custom-call | tf_op jit(solution)/shard_map/cayley_two/pallas_call | solution.py:279
  169.1 5.6 %combine.3.refs_6_ = f32[2048,512]{1,0:T(8,128)} custom-call(s32[1]{0:T(128)} %bitcast.at_ref, f32[1024,256]{1,0:T(8,128)} %copy-done.3, f32[512,256]{1,0:T(8,128)} %collective-permute-done.1.refs_0_.refs_1_, f32[512,256]{1,0:T(8,128)} %collective-permute-done.left_ref.refs_2_, f32[1024,256]{1,0:T(8,128)} %rotate.11.refs_1_.refs_3_, ...), custom_call_target="tpu_custom_call" | custom-call | tf_op jit(solution)/shard_map/combine/pallas_call | solution.py:346
  174.7 1.6 collective-permute-done.7.refs_3_
  176.4 0.0 collective-permute-done.6.refs_2_
  176.4 4.4 %combine.4.refs_4_ = f32[2048,512]{1,0:T(8,128)} custom-call(s32[1]{0:T(128)S(6)} %sub.4.at_ref, f32[1024,256]{1,0:T(8,128)} %rotate.10.refs_0_, f32[512,256]{1,0:T(8,128)} %rotate.8.refs_1_, f32[1024,256]{1,0:T(8,128)} %collective-permute-done.6.refs_2_, f32[512,256]{1,0:T(8,128)} %collective-permute-done.7.refs_3_, ...), custom_call_target="tpu_custom_call", output_to_operand_aliasing={{}: (7, {})} | custom-call | tf_op jit(solution)/shard_map/combine/pallas_call | solution.py:346
  180.8 1.1 collective-permute-done.5.refs_1_
  181.9 0.8 copy-done.6
  182.7 2.7 %combine.5 = f32[2048,512]{1,0:T(8,128)} custom-call(s32[1]{0:T(128)S(6)} %sub.4.at_ref, f32[512,256]{1,0:T(8,128)} %rotate.6.refs_0_, f32[512,256]{1,0:T(8,128)} %copy-done.6, bf16[512,256]{1,0:T(8,128)(2,1)} %get-tuple-element.37.refs_4_.refs_2_, bf16[512,256]{1,0:T(8,128)(2,1)} %get-tuple-element.38.refs_5_.refs_3_, ...), custom_call_target="tpu_custom_call", output_to_operand_aliasing={{}: (5, {})} | custom-call | tf_op jit(solution)/shard_map/combine/pallas_call | solution.py:346
  (12 shorter events, 0.0 us)
Async XLA Ops:
  29.8 15.8 %all-to-all-start.1 = ((f32[16,16,256]{2,1,0:T(8,128)}), f32[16,16,256]{2,1,0:T(8,128)S(1)}, u32[]{:S(2)}, u32[]{:S(2)}) async-start(f32[16,16,256]{2,1,0:T(8,128)} %get-tuple-element.24), calls=%async_computation.1 | async-start | bytes 524288 | tf_op jit(solution)/shard_map/all_to_all | solution.py:361
  45.6 0.7 copy-start.5
  56.5 33.2 %collective-permute-start.2 = (f32[1024,256]{1,0:T(8,128)}, f32[1024,256]{1,0:T(8,128)S(1)}, u32[]{:S(2)}, u32[]{:S(2)}) collective-permute-start(f32[1024,256]{1,0:T(8,128)} %rotate.10.refs_0_), channel_id=1, source_target_pairs={{0,2},{2,4},{4,6},{6,8},{8,10},{10,12},{12,14},{14,15},{15,13},{13... | collective-permute-start | bytes 3145736 | tf_op jit(solution)/shard_map/ppermute | solution.py:390
  59.9 35.4 %collective-permute-start.1 = (f32[512,256]{1,0:T(8,128)}, f32[512,256]{1,0:T(8,128)}, u32[]{:S(2)}, u32[]{:S(2)}) collective-permute-start(f32[512,256]{1,0:T(8,128)} %rotate.8.refs_1_), channel_id=1, source_target_pairs={{0,2},{2,4},{4,6},{6,8},{8,10},{10,12},{12,14},{14,15},{15,13},{13... | collective-permute-start | bytes 1572872 | tf_op jit(solution)/shard_map/ppermute | solution.py:390
  64.6 36.3 %collective-permute-start = (f32[512,256]{1,0:T(8,128)}, f32[512,256]{1,0:T(8,128)}, u32[]{:S(2)}, u32[]{:S(2)}) collective-permute-start(f32[512,256]{1,0:T(8,128)} %rotate.6.refs_0_), channel_id=1, source_target_pairs={{0,2},{2,4},{4,6},{6,8},{8,10},{10,12},{12,14},{14,15},{15,13},{13... | collective-permute-start | bytes 1572872 | tf_op jit(solution)/shard_map/ppermute | solution.py:390
  74.1 61.1 %copy-start = (f32[1024,256]{1,0:T(8,128)S(1)}, f32[1024,256]{1,0:T(8,128)}, u32[]{:S(2)}) copy-start(f32[1024,256]{1,0:T(8,128)} %rotate.11.refs_1_.refs_3_) | copy-start | bytes 3145732
  74.1 67.3 %copy-start.2 = (f32[512,256]{1,0:T(8,128)S(1)}, f32[512,256]{1,0:T(8,128)}, u32[]{:S(2)}) copy-start(f32[512,256]{1,0:T(8,128)} %rotate.9.refs_1_.refs_4_) | copy-start | bytes 1572868
  74.1 68.5 %copy-start.1 = (f32[512,256]{1,0:T(8,128)S(1)}, f32[512,256]{1,0:T(8,128)}, u32[]{:S(2)}) copy-start(f32[512,256]{1,0:T(8,128)} %rotate.7.right_ref.refs_5_) | copy-start | bytes 1572868
  89.7 1.0 copy-start.3
  124.2 4.3 %collective-permute-start.3 = (f32[40,256]{1,0:T(8,128)}, f32[40,256]{1,0:T(8,128)S(1)}, u32[]{:S(2)}, u32[]{:S(2)}) collective-permute-start(f32[40,256]{1,0:T(8,128)} %get-tuple-element.32.mine_ref), channel_id=1, source_target_pairs={{2,0},{4,2},{6,4},{8,6},{10,8},{12,10},{14,12},{15,14},{13,15},{11... | collective-permute-start | bytes 122888 | tf_op jit(solution)/shard_map/ppermute | solution.py:405
  128.4 7.6 %copy-start.7 = (f32[40,256]{1,0:T(8,128)}, f32[40,256]{1,0:T(8,128)S(1)}, u32[]{:S(2)}) copy-start(f32[40,256]{1,0:T(8,128)S(1)} %collective-permute-done.3.other_ref) | copy-start | bytes 122884
  129.2 6.0 %collective-permute-start.4 = (f32[80,256]{1,0:T(8,128)S(1)}, f32[80,256]{1,0:T(8,128)S(1)}, u32[]{:S(2)}, u32[]{:S(2)}) collective-permute-start(f32[80,256]{1,0:T(8,128)S(1)} %pad_maximum_fusion), channel_id=1, source_target_pairs={{0,128},{16,144},{32,160},{48,176},{64,192},{80,208},{96,224},{112... | collective-permute-start | bytes 245768 | tf_op jit(solution)/shard_map/ppermute | solution.py:406
  135.2 0.8 copy-start.8
  135.2 41.1 %collective-permute-start.6 = (f32[1024,256]{1,0:T(8,128)S(1)}, f32[1024,256]{1,0:T(8,128)}, u32[]{:S(2)}, u32[]{:S(2)}) collective-permute-start(f32[1024,256]{1,0:T(8,128)S(1)} %copy-done), channel_id=1, source_target_pairs={{2,0},{4,2},{6,4},{8,6},{10,8},{12,10},{14,12},{15,14},{13,15},{11... | collective-permute-start | bytes 3145736 | tf_op jit(solution)/shard_map/ppermute | solution.py:408
  137.8 19.3 %all-to-all-start.3 = ((f32[8,64,256]{2,1,0:T(8,128)}), f32[8,64,256]{2,1,0:T(8,128)S(1)}, u32[]{:S(2)}, u32[]{:S(2)}) async-start(f32[8,64,256]{2,1,0:T(8,128)} %get-tuple-element.34), calls=%async_computation.3 | async-start | bytes 1048576 | tf_op jit(solution)/shard_map/all_to_all | solution.py:361
  141.3 35.0 %collective-permute-start.7 = (f32[512,256]{1,0:T(8,128)S(1)}, f32[512,256]{1,0:T(8,128)}, u32[]{:S(2)}, u32[]{:S(2)}) collective-permute-start(f32[512,256]{1,0:T(8,128)S(1)} %copy-done.2), channel_id=1, source_target_pairs={{2,0},{4,2},{6,4},{8,6},{10,8},{12,10},{14,12},{15,14},{13,15},{11... | collective-permute-start | bytes 1572872 | tf_op jit(solution)/shard_map/ppermute | solution.py:402
  142.6 39.3 %collective-permute-start.5 = (f32[512,256]{1,0:T(8,128)S(1)}, f32[512,256]{1,0:T(8,128)S(1)}, u32[]{:S(2)}, u32[]{:S(2)}) collective-permute-start(f32[512,256]{1,0:T(8,128)S(1)} %copy-done.1), channel_id=1, source_target_pairs={{2,0},{4,2},{6,4},{8,6},{10,8},{12,10},{14,12},{15,14},{13,15},{11... | collective-permute-start | bytes 1572872 | tf_op jit(solution)/shard_map/ppermute | solution.py:408
  157.2 0.8 copy-start.4
  181.9 0.8 copy-start.6

commit v3 on v2

--- a/solution.py
+++ b/solution.py
@@ -9,6 +9,7 @@
 F32, BF16 = jnp.float32, jnp.bfloat16
 TAIL = 8
 LANES = 128
+BLOCK = 512
 
 
 def halves(x):
@@ -144,26 +145,24 @@
     )(slabs)
 
 
-def paired(mine, other, partner, peers, per):
+def paired(mine, partner, other, far, peers, per):
     cols = mine.shape[1]
 
-    def kernel(mine_ref, other_ref, partner_ref, out_ref, norms_ref, other_norms_ref):
-        sums = []
-        for edge, ref in enumerate((mine_ref, other_ref)):
-            begin = edge * (per + TAIL)
-            sums.append(ref[...] + partner_ref[begin : begin + per + TAIL])
+    def kernel(mine_ref, partner_ref, other_ref, far_ref, out_ref, norms_ref, other_norms_ref):
+        own = mine_ref[...] + partner_ref[...]
+        theirs = other_ref[...] + far_ref[...]
         for peer in range(peers):
-            out_ref[peer, :per] = sums[0][:per]
-            out_ref[peer, per:] = sums[1][:per]
-        norms_ref[...] = sums[0][per:]
-        other_norms_ref[...] = sums[1][per:]
+            out_ref[peer, :per] = own[:per]
+            out_ref[peer, per:] = theirs[:per]
+        norms_ref[...] = own[per:]
+        other_norms_ref[...] = theirs[per:]
 
     norms = jax.ShapeDtypeStruct((TAIL, cols), F32)
     return pl.pallas_call(
         kernel,
         out_shape=(jax.ShapeDtypeStruct((peers, 2 * per, cols), F32), norms, norms),
         name="paired",
-    )(mine, other, partner)
+    )(mine, partner, other, far)
 
 
 def cayley(edges, rows_all, power_refs, inverse_refs):
@@ -233,10 +232,13 @@
     low_ref[at_row : at_row + rows, at_col : at_col + cols] = low
 
 
-def step_one_matrices(gathered, norms, swap, rows_all):
+def step_one_matrices(gathered, norms, swap, matrix, rows, rows_all):
     cols = gathered.shape[2]
 
-    def kernel(swap_ref, cross_ref, norms_ref, high_ref, low_ref, power_ref, inverse_ref):
+    def kernel(swap_ref, cross_ref, norms_ref, x_in, high_ref, low_ref, first_ref, *refs):
+        power_ref, inverse_ref, x_ref, sem = refs
+        copy = pltpu.make_async_copy(x_in.at[pl.ds(0, rows), :], x_ref, sem)
+        copy.start()
         cross = cross_ref[...].reshape(cols, cols)
         edge = (cross, norms_ref[...], 1.0)
         blocks = cayley([edge], rows_all, [power_ref], [inverse_ref])[0]
@@ -245,44 +247,119 @@
             near, far = blocks[2 * line], blocks[2 * line + 1]
             store_halves(high_ref, low_ref, line * cols, 0, jnp.where(turned, far, near))
             store_halves(high_ref, low_ref, line * cols, cols, jnp.where(turned, near, far))
+        copy.wait()
+        x_high, x_low = halves(x_ref[...])
+        m_high, m_low = high_ref[:, :cols], low_ref[:, :cols]
+        first_ref[...] = product(x_high, m_high) + (
+            product(x_high, m_low) + product(x_low, m_high)
+        )
 
     out = jax.ShapeDtypeStruct((2 * cols, 2 * cols), BF16)
     vmem = pl.BlockSpec(memory_space=pltpu.VMEM)
     return pl.pallas_call(
         kernel,
-        in_specs=[pl.BlockSpec(memory_space=pltpu.SMEM), vmem, vmem],
-        out_shape=(out, out),
-        scratch_shapes=[pltpu.VMEM((cols, cols), F32)] * 2,
+        in_specs=[
+            pl.BlockSpec(memory_space=pltpu.SMEM),
+            vmem,
+            vmem,
+            pl.BlockSpec(memory_space=pl.ANY),
+        ],
+        out_shape=(out, out, jax.ShapeDtypeStruct((rows, cols), F32)),
+        scratch_shapes=[
+            pltpu.VMEM((cols, cols), F32),
+            pltpu.VMEM((cols, cols), F32),
+            pltpu.VMEM((rows, 2 * cols), F32),
+            pltpu.SemaphoreType.DMA,
+        ],
         name="cayley_one",
-    )(swap, gathered, norms)
-
-
-def step_two_matrices(gathered, norms, other_norms, marks, rows_all):
+    )(swap, gathered, norms, matrix)
+
+
+def step_two(gathered, norms, other_norms, marks, received, sent, rows, rows_all, block):
     _, both, cols = gathered.shape
     per = both // 2
+    pieces = [(0, *p) for p in received] + [(1, *p) for p in sent]
+    places = [
+        (edge, k, row, n * block)
+        for k, (edge, row, left, _) in enumerate(pieces)
+        for n in range(left.shape[0] // block)
+    ]
+    blocks = len(places)
 
     def kernel(marks_ref, cross_ref, norms_ref, other_ref, *refs):
-        outs, power_refs, inverse_refs = refs[:4], refs[4:6], refs[6:]
+        ins = refs[: 2 * len(pieces)]
+        out_ref, high_ref, low_ref = refs[2 * len(pieces) : 2 * len(pieces) + 3]
+        power_refs, inverse_refs = refs[-10:-8], refs[-8:-6]
+        data_ref, turned_ref, own_high, own_low, in_sems, out_sems = refs[-6:]
+        loads = []
+        for i, (_, k, _, begin) in enumerate(places):
+            for side in range(2):
+                load = pltpu.make_async_copy(
+                    ins[2 * k + side].at[pl.ds(begin, block), :],
+                    data_ref.at[i, :, pl.ds(side * cols, cols)],
+                    in_sems.at[2 * i + side],
+                )
+                load.start()
+                loads.append(load)
         edges = []
         for edge in range(2):
             cross = cross_ref[:, edge * per : (edge + 1) * per, :].reshape(cols, cols)
             sign = jnp.where(marks_ref[2 * edge] != 0, 1.0, -1.0).astype(F32)
             edges.append((cross, (norms_ref, other_ref)[edge][...], sign))
-        for edge, blocks in enumerate(cayley(edges, rows_all, power_refs, inverse_refs)):
+        matrices = ((own_high, own_low), (high_ref, low_ref))
+        for edge, turns in enumerate(cayley(edges, rows_all, power_refs, inverse_refs)):
             moved_role = marks_ref[2 * edge + 1] != 0
-            for line in range(2):
-                value = jnp.where(moved_role, blocks[2 * line], blocks[2 * line + 1])
-                store_halves(outs[2 * edge], outs[2 * edge + 1], line * cols, 0, value)
+            for half in range(2):
+                value = jnp.where(moved_role, turns[2 * half], turns[2 * half + 1])
+                store_halves(*matrices[edge], half * cols, 0, value)
+        columns = [
+            pl.multiple_of(marks_ref[4] * cols, cols),
+            pl.multiple_of((1 - marks_ref[4]) * cols, cols),
+        ]
+        stores = []
+        for i, (edge, _, row, begin) in enumerate(places):
+            loads[2 * i].wait()
+            loads[2 * i + 1].wait()
+            x_high, x_low = halves(data_ref[i])
+            m_high, m_low = matrices[edge]
+            turned_ref[i] = product(x_high, m_high[...]) + (
+                product(x_high, m_low[...]) + product(x_low, m_high[...])
+            )
+            store = pltpu.make_async_copy(
+                turned_ref.at[i],
+                out_ref.at[pl.ds(row + begin, block), pl.ds(columns[edge], cols)],
+                out_sems.at[i],
+            )
+            store.start()
+            stores.append(store)
+        for store in stores:
+            store.wait()
 
     out = jax.ShapeDtypeStruct((2 * cols, cols), BF16)
     vmem = pl.BlockSpec(memory_space=pltpu.VMEM)
-    return pl.pallas_call(
-        kernel,
-        in_specs=[pl.BlockSpec(memory_space=pltpu.SMEM), vmem, vmem, vmem],
-        out_shape=(out,) * 4,
-        scratch_shapes=[pltpu.VMEM((cols, cols), F32)] * 4,
-        name="cayley_two",
-    )(marks, gathered, norms, other_norms)
+    anywhere = pl.BlockSpec(memory_space=pl.ANY)
+    return pl.pallas_call(
+        kernel,
+        in_specs=[
+            pl.BlockSpec(memory_space=pltpu.SMEM),
+            vmem,
+            vmem,
+            vmem,
+            *[anywhere] * (2 * len(pieces)),
+        ],
+        out_specs=(anywhere, vmem, vmem),
+        out_shape=(jax.ShapeDtypeStruct((rows, 2 * cols), F32), out, out),
+        scratch_shapes=[
+            *[pltpu.VMEM((cols, cols), F32)] * 4,
+            pltpu.VMEM((blocks, block, 2 * cols), F32),
+            pltpu.VMEM((blocks, block, cols), F32),
+            pltpu.VMEM((2 * cols, cols), BF16),
+            pltpu.VMEM((2 * cols, cols), BF16),
+            pltpu.SemaphoreType.DMA((2 * blocks,)),
+            pltpu.SemaphoreType.DMA((blocks,)),
+        ],
+        name="step_two",
+    )(marks, gathered, norms, other_norms, *[x for p in pieces for x in p[2:]])
 
 
 def rotate(both, high, low, part, start, rows, block=512):
@@ -377,53 +454,62 @@
     clockwise = [(ring[i], ring[(i + 1) % size]) for i in range(size)]
     back = [(b, a) for a, b in clockwise]
     even = position % 2 == 0
-    pieces = [(0, rows // 2), (rows // 2, rows // 4), (3 * rows // 4, rows // 4)]
+    pieces = [(0, rows // 4), (rows // 4, rows // 2), (3 * rows // 4, rows // 4)]
 
     slabs = exchanged(gram(matrix, 0, matrix, 1, rows, peers, cols, block=rows // 2))
     spread, norms = slab_sum(slabs, cols, True)
     gathered = exchanged(spread)
     swap = jnp.where(even & (position > 0), 0, 1).astype(jnp.int32)[None]
-    high, low = step_one_matrices(gathered, norms, swap, float(rows_all))
-    onward, arrived = [], []
+    high, low, turned = step_one_matrices(
+        gathered, norms, swap, matrix, pieces[0][1], float(rows_all)
+    )
+    onward, arrived = [turned], []
     for k, piece in enumerate(pieces):
-        onward.append(rotate(matrix, high, low, 0, *piece))
+        if k:
+            onward.append(rotate(matrix, high, low, 0, *piece))
         arrived.append(lax.ppermute(onward[k], "pairs", clockwise))
     kept = [rotate(matrix, high, low, 1, *piece) for piece in pieces]
 
     line = peers // 2
     halves_of_rows = [[*range(line)], [*range(line, peers)]]
     across = [(i, (i + line) % peers) for i in range(peers)]
+    both_ways = [(r * size + b, q * size + a) for r, q in across for b, a in back]
     per = cols // line
     begun = ()
     for k in range(2):
         begun = gram_parts(arrived[k : k + 1], kept[k : k + 1], cols, begun)
     slabs = gram(arrived[2], 0, kept[2], 0, pieces[2][1], line, cols, begun)
     returned = [None] * 3
-    returned[1] = lax.ppermute(held(kept[1], slabs), "pairs", back)
+    returned[0] = lax.ppermute(held(kept[0], slabs), "pairs", back)
     slabs = exchanged(slabs, halves_of_rows)
     mine, _ = slab_sum(slabs, cols, False)
     other = lax.ppermute(mine, "pairs", back)
-    partner = lax.ppermute(jnp.concatenate([mine, other], axis=0), "rows", across)
-    for at in (0, 2):
-        returned[at] = lax.ppermute(held(kept[at], partner), "pairs", back)
-    pair, norms, other_norms = paired(mine, other, partner, line, per)
+    partner = lax.ppermute(mine, "rows", across)
+    far = lax.ppermute(mine, ("rows", "pairs"), both_ways)
+    for at in (2, 1):
+        returned[at] = lax.ppermute(held(kept[at], far, partner, other), "pairs", back)
+    pair, norms, other_norms = paired(mine, partner, other, far, line, per)
     gathered = exchanged(pair, halves_of_rows)
+    in_second = ~even
     marks = jnp.stack(
         [
             (even & (position > 0)) | (position == size - 1),
             position != 0,
             even,
             position == 1,
+            in_second,
         ]
     ).astype(jnp.int32)
-    matrices = step_two_matrices(gathered, norms, other_norms, marks, float(rows_all))
-    in_first = jnp.where(even, 0, 1).astype(jnp.int32)[None]
-    done = combine(in_first, arrived, kept, *matrices[:2], 0, rows)
-    for k in (slice(0, 2), slice(2, 3)):
-        done = combine(
-            1 - in_first, onward[k], returned[k], *matrices[2:], pieces[k.start][0], rows, done
-        )
-    return done
+    begins = [begin for begin, _ in pieces]
+    received = list(zip(begins, arrived, kept))
+    sent = [(begins[k], onward[k], returned[k]) for k in (0, 2)]
+    done, high, low = step_two(
+        gathered, norms, other_norms, marks, received, sent, rows, float(rows_all), BLOCK
+    )
+    in_first = even.astype(jnp.int32)[None]
+    return combine(
+        in_first, onward[1:2], returned[1:2], high, low, begins[1], rows, done
+    )
 
 
 def solution(mesh):

time: 186 us -> 203 us (1.091)
  the two profiles are of different devices: /device:TPU:4 before, /device:TPU:44 now
where the time goes in v3:
time: 203 us; the launch traced here: 199 us
  waiting for transfers between devices  78.3 us (39%)
  Pallas kernels  60.6 us (30%)
  blocking collectives  37.8 us (19%)
  starting transfers between devices  19.2 us (9%)
  local copies, waits for them, and re-layouts  2.69 us (1%)
    all_to_all x2, blocking collectives, exchanged(): lax.all_to_all(blocks, 'rows', 0, 0, axis_index_groups=groups, tiled=True)  37.8 us
    ppermute x1, waiting for transfers between devices, shards(): returned[0] = lax.ppermute(held(kept[0], slabs), 'pairs', back)  29.9 us
    ppermute x3, waiting for transfers between devices, shards(): arrived.append(lax.ppermute(onward[k], 'pairs', clockwise))  26.8 us
    pallas_call x1, Pallas kernels, step_two(): pl.pallas_call(kernel, in_specs=[pl.BlockSpec(memory_space=pltpu.SMEM), v...  18.3 us
    pallas_call x5, Pallas kernels, rotate(): pl.pallas_call(kernel, grid=(rows // block,), in_specs=[pl.BlockSpec((blo...  14.9 us
    all_to_all x2, waiting for transfers between devices, exchanged(): lax.all_to_all(blocks, 'rows', 0, 0, axis_index_groups=groups, tiled=True)  11.3 us
    all_to_all x2, starting transfers between devices, exchanged(): lax.all_to_all(blocks, 'rows', 0, 0, axis_index_groups=groups, tiled=True)  10 us
    pallas_call x1, Pallas kernels, step_one_matrices(): pl.pallas_call(kernel, in_specs=[pl.BlockSpec(memory_space=pltpu.SMEM), v...  7.35 us
  transfers between devices with their start and end apart: 11, of which 7 were waited for; matrix products, arithmetic and copies ran while one was open for 0% of the time, Pallas kernels for 19%

profile of v3, /device:TPU:44, one launch (start us, length us, event | category | flops | bytes accessed | tf_op | source)
XLA Modules:
  0.0 199.1 jit_solution(12459422449182684179)
XLA Ops:
  0.0 3.8 %gram.2 = f32[16,40,128]{2,1,0:T(8,128)} custom-call(f32[2048,512]{1,0:T(8,128)} %x_ref.9, f32[2048,512]{1,0:T(8,128)} %x_ref.9), custom_call_target="tpu_custom_call" | custom-call | tf_op jit(solution)/shard_map/gram/pallas_call | solution.py:101
  3.8 23.1 %all_to_all.20.in_ref = f32[16,40,128]{2,1,0:T(8,128)} all-to-all(f32[16,40,128]{2,1,0:T(8,128)} %gram.2), channel_id=1, replica_groups=mesh['rows'=16,'pairs'=16] {'rows'}, dimensions={0} | all-to-all | bytes 655360 | tf_op jit(solution)/shard_map/all_to_all | solution.py:438
  26.9 1.7 slab_sum.2
  28.6 4.9 %all-to-all-start.1 = ((f32[16,16,256]{2,1,0:T(8,128)}), f32[16,16,256]{2,1,0:T(8,128)S(1)}, u32[]{:S(2)}, u32[]{:S(2)}) async-start(f32[16,16,256]{2,1,0:T(8,128)} %get-tuple-element.24), calls=%async_computation.1 | async-start | bytes 524288 | tf_op jit(solution)/shard_map/all_to_all | solution.py:438
  33.5 11.3 %all-to-all-done.1.cross_ref = f32[16,16,256]{2,1,0:T(8,128)S(1)} async-done(((f32[16,16,256]{2,1,0:T(8,128)}), f32[16,16,256]{2,1,0:T(8,128)S(1)}, u32[]{:S(2)}, u32[]{:S(2)}) %all-to-all-start.1) | async-done | bytes 262176 | tf_op jit(solution)/shard_map/all_to_all | solution.py:438
  44.8 0.7 copy-done.5
  45.6 7.3 %cayley_one.1 = (bf16[512,512]{1,0:T(8,128)(2,1)}, bf16[512,512]{1,0:T(8,128)(2,1)}, f32[512,256]{1,0:T(8,128)}) custom-call(s32[1]{0:T(128)} %bitcast.1.swap_ref, f32[16,16,256]{2,1,0:T(8,128)} %copy-done.5, f32[8,256]{1,0:T(8,128)} %get-tuple-element.25.norms_ref, f32[2048,512]{1,0:T(8,128)} %x_ref.9), custom_call_target="tpu_custom_call" | custom-call | tf_op jit(solution)/shard_map/cayley_one/pallas_call | solution.py:259
  52.9 3.4 %rotate.5.refs_0_ = f32[1024,256]{1,0:T(8,128)} custom-call(f32[2048,512]{1,0:T(8,128)} %x_ref.9, bf16[512,512]{1,0:T(8,128)(2,1)} %get-tuple-element.26.high_ref, bf16[512,512]{1,0:T(8,128)(2,1)} %get-tuple-element.27.low_ref), custom_call_target="tpu_custom_call" | custom-call | tf_op jit(solution)/shard_map/rotate/pallas_call | solution.py:377
  56.3 2.0 collective-permute-start.1
  58.2 0.7 collective-permute-start.2
  58.9 2.7 %rotate.7.refs_8_ = f32[512,256]{1,0:T(8,128)} custom-call(f32[2048,512]{1,0:T(8,128)} %x_ref.9, bf16[512,512]{1,0:T(8,128)(2,1)} %get-tuple-element.26.high_ref, bf16[512,512]{1,0:T(8,128)(2,1)} %get-tuple-element.27.low_ref), custom_call_target="tpu_custom_call" | custom-call | tf_op jit(solution)/shard_map/rotate/pallas_call | solution.py:377
  61.7 0.0 collective-permute-start
  61.7 2.7 %rotate.9.refs_1_ = f32[512,256]{1,0:T(8,128)} custom-call(f32[2048,512]{1,0:T(8,128)} %x_ref.9, bf16[512,512]{1,0:T(8,128)(2,1)} %get-tuple-element.26.high_ref, bf16[512,512]{1,0:T(8,128)(2,1)} %get-tuple-element.27.low_ref), custom_call_target="tpu_custom_call" | custom-call | tf_op jit(solution)/shard_map/rotate/pallas_call | solution.py:377
  64.4 2.7 %rotate.8.right_ref.refs_5_ = f32[512,256]{1,0:T(8,128)} custom-call(f32[2048,512]{1,0:T(8,128)} %x_ref.9, bf16[512,512]{1,0:T(8,128)(2,1)} %get-tuple-element.26.high_ref, bf16[512,512]{1,0:T(8,128)(2,1)} %get-tuple-element.27.low_ref), custom_call_target="tpu_custom_call" | custom-call | tf_op jit(solution)/shard_map/rotate/pallas_call | solution.py:377
  67.1 3.3 %rotate.6.refs_1_.refs_3_ = f32[1024,256]{1,0:T(8,128)} custom-call(f32[2048,512]{1,0:T(8,128)} %x_ref.9, bf16[512,512]{1,0:T(8,128)(2,1)} %get-tuple-element.26.high_ref, bf16[512,512]{1,0:T(8,128)(2,1)} %get-tuple-element.27.low_ref), custom_call_target="tpu_custom_call" | custom-call | tf_op jit(solution)/shard_map/rotate/pallas_call | solution.py:377
  70.5 26.8 %collective-permute-done.2.refs_0_ = f32[512,256]{1,0:T(8,128)} collective-permute-done((f32[512,256]{1,0:T(8,128)}, f32[512,256]{1,0:T(8,128)}, u32[]{:S(2)}, u32[]{:S(2)}) %collective-permute-start.2) | collective-permute-done | bytes 524320 | tf_op jit(solution)/shard_map/ppermute | solution.py:470
  97.2 2.4 %gram_parts.2 = (f32[256,256]{1,0:T(8,128)}, f32[8,512]{1,0:T(8,128)}) custom-call(f32[512,256]{1,0:T(8,128)} %collective-permute-done.2.refs_0_, f32[512,256]{1,0:T(8,128)} %rotate.9.refs_1_), custom_call_target="tpu_custom_call" | custom-call | tf_op jit(solution)/shard_map/gram_parts/pallas_call | solution.py:53
  99.6 0.0 collective-permute-done.1.refs_0_.refs_2_
  99.6 1.0 copy-done.3
  100.6 3.0 %gram_parts.3 = (f32[256,256]{1,0:T(8,128)}, f32[8,512]{1,0:T(8,128)}) custom-call(f32[1024,256]{1,0:T(8,128)} %copy-done.3, f32[1024,256]{1,0:T(8,128)} %rotate.6.refs_1_.refs_3_, f32[256,256]{1,0:T(8,128)} %get-tuple-element.29.refs_2_, f32[8,512]{1,0:T(8,128)} %get-tuple-element.30.refs_3_), custom_call_target="tpu_custom_call" | custom-call | tf_op jit(solution)/shard_map/gram_parts/pallas_call | solution.py:53
  103.6 0.0 collective-permute-done.left_ref.refs_4_
  103.6 2.5 %gram.3 = f32[8,72,128]{2,1,0:T(8,128)} custom-call(f32[512,256]{1,0:T(8,128)} %collective-permute-done.left_ref.refs_4_, f32[512,256]{1,0:T(8,128)} %rotate.8.right_ref.refs_5_, f32[256,256]{1,0:T(8,128)} %get-tuple-element.31.refs_0_, f32[8,512]{1,0:T(8,128)} %get-tuple-element.32.refs_1_), custom_call_target="tpu_custom_call" | custom-call | tf_op jit(solution)/shard_map/gram/pallas_call | solution.py:101
  106.1 14.7 %all_to_all.21.in_ref = f32[8,72,128]{2,1,0:T(8,128)} all-to-all(f32[8,72,128]{2,1,0:T(8,128)} %gram.3), channel_id=1, replica_groups={{0,16,32,48,64,80,96,112},{128,144,160,176,192,208,224,240},{1,17,33,49..., dimensions={0} | all-to-all | bytes 589824 | tf_op jit(solution)/shard_map/all_to_all | solution.py:438
  120.8 1.6 slab_sum.3
  122.4 2.2 %collective-permute-start.5 = (f32[40,256]{1,0:T(8,128)}, f32[40,256]{1,0:T(8,128)S(1)}, u32[]{:S(2)}, u32[]{:S(2)}) collective-permute-start(f32[40,256]{1,0:T(8,128)} %get-tuple-element.33.mine_ref), channel_id=1, source_target_pairs={{2,0},{4,2},{6,4},{8,6},{10,8},{12,10},{14,12},{15,14},{13,15},{11... | collective-permute-start | bytes 122888 | tf_op jit(solution)/shard_map/ppermute | solution.py:486
  124.5 0.8 collective-permute-start.4
  125.3 0.7 collective-permute-start.3
  126.0 1.5 collective-permute-done.5.other_ref
  127.5 3.1 %collective-permute-done.4.partner_ref = f32[40,256]{1,0:T(8,128)S(1)} collective-permute-done((f32[40,256]{1,0:T(8,128)}, f32[40,256]{1,0:T(8,128)S(1)}, u32[]{:S(2)}, u32[]{:S(2)}) %collective-permute-start.4) | collective-permute-done | bytes 40992 | tf_op jit(solution)/shard_map/ppermute | solution.py:487
  130.5 0.2 collective-permute-done.3.far_ref
  130.7 0.0 copy-done
  130.7 0.8 collective-permute-start.6
  131.5 0.0 copy-done.7
  131.5 0.0 copy-done.8
  131.5 0.0 copy-done.9
  131.5 1.7 paired.1
  133.2 5.1 %all-to-all-start.3 = ((f32[8,64,256]{2,1,0:T(8,128)}), f32[8,64,256]{2,1,0:T(8,128)S(1)}, u32[]{:S(2)}, u32[]{:S(2)}) async-start(f32[8,64,256]{2,1,0:T(8,128)} %get-tuple-element.35), calls=%async_computation.3 | async-start | bytes 1048576 | tf_op jit(solution)/shard_map/all_to_all | solution.py:438
  138.3 0.9 collective-permute-start.7
  139.2 1.2 collective-permute-start.8
  140.4 0.1 stack.20
  140.5 0.5 convert_element_type.4.marks_ref
  141.0 29.9 %collective-permute-done.7.refs_7_ = f32[512,256]{1,0:T(8,128)S(1)} collective-permute-done((f32[512,256]{1,0:T(8,128)S(1)}, f32[512,256]{1,0:T(8,128)S(1)}, u32[]{:S(2)}, u32[]{:S(2)}) %collective-permute-start.7) | collective-permute-done | bytes 524320 | tf_op jit(solution)/shard_map/ppermute | solution.py:483
  170.9 5.6 %collective-permute-done.8.refs_9_ = f32[512,256]{1,0:T(8,128)} collective-permute-done((f32[512,256]{1,0:T(8,128)S(1)}, f32[512,256]{1,0:T(8,128)}, u32[]{:S(2)}, u32[]{:S(2)}) %collective-permute-start.8) | collective-permute-done | bytes 524320 | tf_op jit(solution)/shard_map/ppermute | solution.py:490
  176.5 0.0 all-to-all-done.3.cross_ref
  176.5 0.9 copy-done.4
  177.3 18.3 %step_two.1 = (f32[2048,512]{1,0:T(8,128)}, bf16[512,256]{1,0:T(8,128)(2,1)}, bf16[512,256]{1,0:T(8,128)(2,1)}) custom-call(s32[5]{0:T(128)} %convert_element_type.4.marks_ref, f32[8,64,256]{2,1,0:T(8,128)} %copy-done.4, f32[8,256]{1,0:T(8,128)} %get-tuple-element.36.norms_ref, f32[8,256]{1,0:T(8,128)} %get-tuple-element.37.other_ref, ...), custom_call_target="tpu_custom_call" | custom-call | tf_op jit(solution)/shard_map/step_two/pallas_call | solution.py:341
  195.7 0.0 collective-permute-done.6.refs_1_
  195.7 3.4 %combine.1 = f32[2048,512]{1,0:T(8,128)} custom-call(s32[1]{0:T(128)S(6)} %broadcast_in_dim.9.at_ref, f32[1024,256]{1,0:T(8,128)} %rotate.5.refs_0_, f32[1024,256]{1,0:T(8,128)} %collective-permute-done.6.refs_1_, bf16[512,256]{1,0:T(8,128)(2,1)} %get-tuple-element.40.refs_2_, ...), custom_call_target="tpu_custom_call", output_to_operand_aliasing={{}: (5, {})} | custom-call | tf_op jit(solution)/shard_map/combine/pallas_call | solution.py:423
  (13 shorter events, 0.0 us)
Async XLA Ops:
  28.6 16.2 %all-to-all-start.1 = ((f32[16,16,256]{2,1,0:T(8,128)}), f32[16,16,256]{2,1,0:T(8,128)S(1)}, u32[]{:S(2)}, u32[]{:S(2)}) async-start(f32[16,16,256]{2,1,0:T(8,128)} %get-tuple-element.24), calls=%async_computation.1 | async-start | bytes 524288 | tf_op jit(solution)/shard_map/all_to_all | solution.py:438
  44.8 0.7 copy-start.5
  56.3 43.3 %collective-permute-start.1 = (f32[1024,256]{1,0:T(8,128)}, f32[1024,256]{1,0:T(8,128)S(1)}, u32[]{:S(2)}, u32[]{:S(2)}) collective-permute-start(f32[1024,256]{1,0:T(8,128)} %rotate.5.refs_0_), channel_id=1, source_target_pairs={{0,2},{2,4},{4,6},{6,8},{8,10},{10,12},{12,14},{14,15},{15,13},{13... | collective-permute-start | bytes 3145736 | tf_op jit(solution)/shard_map/ppermute | solution.py:470
  58.2 39.0 %collective-permute-start.2 = (f32[512,256]{1,0:T(8,128)}, f32[512,256]{1,0:T(8,128)}, u32[]{:S(2)}, u32[]{:S(2)}) collective-permute-start(f32[512,256]{1,0:T(8,128)} %get-tuple-element.28.refs_6_), channel_id=1, source_target_pairs={{0,2},{2,4},{4,6},{6,8},{8,10},{10,12},{12,14},{14,15},{15,13},{13... | collective-permute-start | bytes 1572872 | tf_op jit(solution)/shard_map/ppermute | solution.py:470
  61.7 42.0 %collective-permute-start = (f32[512,256]{1,0:T(8,128)}, f32[512,256]{1,0:T(8,128)}, u32[]{:S(2)}, u32[]{:S(2)}) collective-permute-start(f32[512,256]{1,0:T(8,128)} %rotate.7.refs_8_), channel_id=1, source_target_pairs={{0,2},{2,4},{4,6},{6,8},{8,10},{10,12},{12,14},{14,15},{15,13},{13... | collective-permute-start | bytes 1572872 | tf_op jit(solution)/shard_map/ppermute | solution.py:470
  70.5 60.2 %copy-start = (f32[1024,256]{1,0:T(8,128)S(1)}, f32[1024,256]{1,0:T(8,128)}, u32[]{:S(2)}) copy-start(f32[1024,256]{1,0:T(8,128)} %rotate.6.refs_1_.refs_3_) | copy-start | bytes 3145732
  70.5 67.8 %copy-start.2 = (f32[512,256]{1,0:T(8,128)S(1)}, f32[512,256]{1,0:T(8,128)}, u32[]{:S(2)}) copy-start(f32[512,256]{1,0:T(8,128)} %rotate.9.refs_1_) | copy-start | bytes 1572868
  70.5 68.8 %copy-start.1 = (f32[512,256]{1,0:T(8,128)S(1)}, f32[512,256]{1,0:T(8,128)}, u32[]{:S(2)}) copy-start(f32[512,256]{1,0:T(8,128)} %rotate.8.right_ref.refs_5_) | copy-start | bytes 1572868
  99.6 1.0 copy-start.3
  122.4 5.1 %collective-permute-start.5 = (f32[40,256]{1,0:T(8,128)}, f32[40,256]{1,0:T(8,128)S(1)}, u32[]{:S(2)}, u32[]{:S(2)}) collective-permute-start(f32[40,256]{1,0:T(8,128)} %get-tuple-element.33.mine_ref), channel_id=1, source_target_pairs={{2,0},{4,2},{6,4},{8,6},{10,8},{12,10},{14,12},{15,14},{13,15},{11... | collective-permute-start | bytes 122888 | tf_op jit(solution)/shard_map/ppermute | solution.py:486
  124.5 6.0 %collective-permute-start.4 = (f32[40,256]{1,0:T(8,128)}, f32[40,256]{1,0:T(8,128)S(1)}, u32[]{:S(2)}, u32[]{:S(2)}) collective-permute-start(f32[40,256]{1,0:T(8,128)} %get-tuple-element.33.mine_ref), channel_id=1, source_target_pairs={{0,128},{16,144},{32,160},{48,176},{64,192},{80,208},{96,224},{112... | collective-permute-start | bytes 122888 | tf_op jit(solution)/shard_map/ppermute | solution.py:487
  125.3 5.4 %collective-permute-start.3 = (f32[40,256]{1,0:T(8,128)}, f32[40,256]{1,0:T(8,128)S(1)}, u32[]{:S(2)}, u32[]{:S(2)}) collective-permute-start(f32[40,256]{1,0:T(8,128)} %get-tuple-element.33.mine_ref), channel_id=1, source_target_pairs={{2,128},{4,130},{6,132},{8,134},{10,136},{12,138},{14,140},{15,142... | collective-permute-start | bytes 122888 | tf_op jit(solution)/shard_map/ppermute | solution.py:488
  127.5 4.0 %copy-start.7 = (f32[40,256]{1,0:T(8,128)}, f32[40,256]{1,0:T(8,128)S(1)}, u32[]{:S(2)}) copy-start(f32[40,256]{1,0:T(8,128)S(1)} %collective-permute-done.5.other_ref) | copy-start | bytes 122884
  130.5 0.9 copy-start.8
  130.7 0.8 copy-start.9
  130.7 65.0 %collective-permute-start.6 = (f32[1024,256]{1,0:T(8,128)S(1)}, f32[1024,256]{1,0:T(8,128)}, u32[]{:S(2)}, u32[]{:S(2)}) collective-permute-start(f32[1024,256]{1,0:T(8,128)S(1)} %copy-done), channel_id=1, source_target_pairs={{2,0},{4,2},{6,4},{8,6},{10,8},{12,10},{14,12},{15,14},{13,15},{11... | collective-permute-start | bytes 3145736 | tf_op jit(solution)/shard_map/ppermute | solution.py:490
  133.2 43.3 %all-to-all-start.3 = ((f32[8,64,256]{2,1,0:T(8,128)}), f32[8,64,256]{2,1,0:T(8,128)S(1)}, u32[]{:S(2)}, u32[]{:S(2)}) async-start(f32[8,64,256]{2,1,0:T(8,128)} %get-tuple-element.35), calls=%async_computation.3 | async-start | bytes 1048576 | tf_op jit(solution)/shard_map/all_to_all | solution.py:438
  138.3 32.6 %collective-permute-start.7 = (f32[512,256]{1,0:T(8,128)S(1)}, f32[512,256]{1,0:T(8,128)S(1)}, u32[]{:S(2)}, u32[]{:S(2)}) collective-permute-start(f32[512,256]{1,0:T(8,128)S(1)} %copy-done.2), channel_id=1, source_target_pairs={{2,0},{4,2},{6,4},{8,6},{10,8},{12,10},{14,12},{15,14},{13,15},{11... | collective-permute-start | bytes 1572872 | tf_op jit(solution)/shard_map/ppermute | solution.py:483
  139.2 37.2 %collective-permute-start.8 = (f32[512,256]{1,0:T(8,128)S(1)}, f32[512,256]{1,0:T(8,128)}, u32[]{:S(2)}, u32[]{:S(2)}) collective-permute-start(f32[512,256]{1,0:T(8,128)S(1)} %copy-done.1), channel_id=1, source_target_pairs={{2,0},{4,2},{6,4},{8,6},{10,8},{12,10},{14,12},{15,14},{13,15},{11... | collective-permute-start | bytes 1572872 | tf_op jit(solution)/shard_map/ppermute | solution.py:490
  170.9 5.6 %copy-start.6 = (f32[512,256]{1,0:T(8,128)}, f32[512,256]{1,0:T(8,128)S(1)}, u32[]{:S(2)}) copy-start(f32[512,256]{1,0:T(8,128)S(1)} %collective-permute-done.7.refs_7_) | copy-start | bytes 1572868
  176.5 0.9 copy-start.4
